TPU v7x, 32 devices: a 4x4x1 block of a 4x4x8 slice. The times are simulated.
32 devices in a mesh: dp: 1 (over z), tp: 32 (over y, x, core).
Axes of the slice: x: 4, y: 4, z: 1, core: 2. Of those that a mesh axis runs over, the one named last changes fastest.
The devices are a block of a 4x4x8 slice.
Arguments:
- x_in: bfloat16 [1, 4096, 2048], P('dp', 'tp')
- ln1_gain: float32 [2, 2048], replicated
- w_qkv: bfloat16 [2, 2048, 32, 192], P(None, None, 'tp')
- w_out: bfloat16 [2, 32, 64, 2048], P(None, 'tp')
- ln2_gain: float32 [2, 2048], replicated
- w_up: bfloat16 [2, 2048, 8192], P(None, None, 'tp')
- w_down: bfloat16 [2, 8192, 2048], P(None, 'tp')
Outputs:
- output: bfloat16 [1, 4096, 2048], P('dp', 'tp')
All inputs are finite; a program needn't handle non-finite values.
Results may differ from a plain program's by a relative error of at most 0.02.
Values are sent between devices in bfloat16 or wider.
A program may use at most 768 MiB of HBM per device.

v0:
```python
import jax
import jax.numpy as jnp
from jax import lax
from jax.sharding import PartitionSpec as P

LN_EPS = 1.0e-5
NEG_BIG = -1.0e30


def layer_norm(residual, ln_gain):
    resid_f32 = residual.astype(jnp.float32)
    row_mean = jnp.mean(resid_f32, axis=-1, keepdims=True)
    centered = resid_f32 - row_mean
    row_var = jnp.mean(centered * centered, axis=-1, keepdims=True)
    return (centered * lax.rsqrt(row_var + LN_EPS) * ln_gain).astype(jnp.bfloat16)


def causal_attention(query_blk, key_blk, value_blk, query_start):
    head_dim = query_blk.shape[-1]
    scores = jnp.einsum('bqhe,bkhe->bhqk', query_blk, key_blk, preferred_element_type=jnp.float32) * head_dim ** -0.5
    query_pos = query_start + jnp.arange(query_blk.shape[1])
    key_pos = jnp.arange(key_blk.shape[1])
    scores = jnp.where(query_pos[:, None] >= key_pos[None, :], scores, NEG_BIG)
    attn_probs = jax.nn.softmax(scores, axis=-1).astype(jnp.bfloat16)
    return jnp.einsum('bhqk,bkhe->bqhe', attn_probs, value_blk, preferred_element_type=jnp.float32).astype(jnp.bfloat16)


def solution(mesh):
    def layer_stack(x_local, ln1_gain, w_qkv, w_out, ln2_gain, w_up, w_down):
        residual = x_local
        head_dim = w_qkv.shape[3] // 3
        for layer_idx in range(w_qkv.shape[0]):
            normed = layer_norm(residual, ln1_gain[layer_idx])
            normed_all = lax.all_gather(normed, 'tp', axis=1, tiled=True)
            qkv_all = jnp.einsum('bsd,dhe->bshe', normed_all, w_qkv[layer_idx], preferred_element_type=jnp.float32).astype(jnp.bfloat16)
            attended = causal_attention(qkv_all[..., :head_dim], qkv_all[..., head_dim:2 * head_dim], qkv_all[..., 2 * head_dim:], 0)
            part_sum = jnp.einsum('bshe,hed->bsd', attended, w_out[layer_idx], preferred_element_type=jnp.float32).astype(jnp.bfloat16)
            reduced = lax.psum_scatter(part_sum, 'tp', scatter_dimension=1, tiled=True)
            residual = (residual.astype(jnp.float32) + reduced.astype(jnp.float32)).astype(jnp.bfloat16)
            normed = layer_norm(residual, ln2_gain[layer_idx])
            normed_all = lax.all_gather(normed, 'tp', axis=1, tiled=True)
            hidden = jax.nn.gelu(jnp.einsum('bsd,df->bsf', normed_all, w_up[layer_idx], preferred_element_type=jnp.float32), approximate=True).astype(jnp.bfloat16)
            part_sum = jnp.einsum('bsf,fd->bsd', hidden, w_down[layer_idx], preferred_element_type=jnp.float32).astype(jnp.bfloat16)
            reduced = lax.psum_scatter(part_sum, 'tp', scatter_dimension=1, tiled=True)
            residual = (residual.astype(jnp.float32) + reduced.astype(jnp.float32)).astype(jnp.bfloat16)
        return residual

    return jax.shard_map(layer_stack, mesh=mesh, in_specs=(P('dp', 'tp', None), P(), P(None, None, 'tp', None), P(None, 'tp', None, None), P(), P(None, None, 'tp'), P(None, 'tp', None)), out_specs=P('dp', 'tp', None), check_vma=False)
```

profile of v0, /device:TPU:97, one launch (start us, length us, event | category | flops | bytes accessed | tf_op | source)
XLA Modules:
  0.0 963.0 jit_solution(16251307200047252058)
XLA Ops:
  6.6 1.2 convert_reduce_fusion.3
  7.8 1.3 fusion.83
  9.1 1.4 fusion.132
  10.5 2.2 fusion.85
  12.8 71.6 %all-gather.5.cloned.1.call-done = bf16[1,4096,2048]{2,1,0:T(8,128)(2,1)} async-done(((bf16[1,128,2048]{2,1,0:T(8,128)(2,1)}), bf16[1,4096,2048]{2,1,0:T(8,128)(2,1)}) %all-gather.5.cloned.1.call-update) | async-done | bytes 16777232 | tf_op jit(solution)/shard_map/all_gather | solution.py:34
  84.4 11.6 %fusion.23 = bf16[1,4096,1,192]{1,3,2,0:T(8,128)(2,1)S(1)} fusion(bf16[1,4096,2048]{2,1,0:T(8,128)(2,1)} %all-gather.5.cloned.1.call-done, bf16[2,2048,1,192]{1,3,2,0:T(8,128)(2,1)} %param.9), kind=kOutput, calls=%fused_computation.30 | convolution fusion | flops 3222011904 | bytes 19136512 | tf_op jit(solution)/shard_map/bsd,dhe->bshe/dot_general | solution.py:35
  96.0 24.4 %fusion.2 = (f32[4096]{0:T(1024)S(1)}, f32[4096,4096]{0,1:T(8,128)}) fusion(bf16[1,4096,1,192]{1,3,2,0:T(8,128)(2,1)S(1)} %fusion.23), kind=kOutput, calls=%fused_computation.9 | convolution fusion | flops 2214588416 | bytes 68173824 | tf_op jit(solution)/shard_map/bqhe,bkhe->bhqk/dot_general | solution.py:20
  120.4 21.8 %fusion = f32[4096]{0:T(1024)S(1)} fusion(f32[4096,4096]{0,1:T(8,128)} %get-tuple-element.16, f32[4096]{0:T(1024)S(1)} %get-tuple-element.15), kind=kLoop, calls=%fused_computation.7 | loop fusion | flops 83881984 | bytes 67141632 | tf_op jit(solution)/shard_map/reduce_sum | solution.py:24
  142.2 34.3 %convert_bitcast_fusion.3 = bf16[1,4096,2048]{2,1,0:T(8,128)(2,1)} fusion(f32[4096,4096]{0,1:T(8,128)} %get-tuple-element.16, f32[4096]{0:T(1024)S(1)} %fusion, f32[4096]{0:T(1024)S(1)} %get-tuple-element.15, bf16[1,4096,1,192]{1,3,2,0:T(8,128)(2,1)S(1)} %fusion.23, bf16[2,1,64,2048]{3,2,1,0:T(8,128)(2,1)S(1)} %copy-done.9), kind=kOutput, calls=%fused_computation.24 | convolution fusion | flops 3330539520 | bytes 84705280 | tf_op jit(solution)/shard_map/bshe,hed->bsd/dot_general | solution.py:37
  176.6 0.6 copy-done.5
  177.2 0.6 fusion.131
  177.8 103.8 %reduce-scatter.5.cloned.1.call-done = bf16[1,128,2048]{2,1,0:T(8,128)(2,1)} async-done(((bf16[1,4096,2048]{2,1,0:T(8,128)(2,1)}), bf16[1,128,2048]{2,1,0:T(8,128)(2,1)}) %reduce-scatter.5.cloned.1.call-update) | async-done | bytes 524304 | tf_op jit(solution)/shard_map/reduce_scatter | solution.py:38
  281.6 1.3 convert_reduce_fusion.2
  283.2 1.2 fusion.82
  284.5 68.7 %all-gather.7.cloned.1.call-done = bf16[1,4096,2048]{2,1,0:T(8,128)(2,1)} async-done(((bf16[1,128,2048]{2,1,0:T(8,128)(2,1)}), bf16[1,4096,2048]{2,1,0:T(8,128)(2,1)}) %all-gather.7.cloned.1.call-update) | async-done | bytes 16777232 | tf_op jit(solution)/shard_map/all_gather | solution.py:41
  353.2 24.7 %convert_bitcast_fusion.2 = bf16[1,4096,2048]{2,1,0:T(8,128)(2,1)} fusion(bf16[1,4096,2048]{2,1,0:T(8,128)(2,1)} %all-gather.7.cloned.1.call-done, bf16[2,256,2048]{2,1,0:T(8,128)(2,1)S(1)} %copy-done.6, bf16[2,2048,256]{2,1,0:T(8,128)(2,1)} %param.12), kind=kOutput, calls=%fused_computation.23 | convolution fusion | flops 8607760384 | bytes 35651584 | tf_op jit(solution)/shard_map/bsf,fd->bsd/dot_general | solution.py:43
  378.0 105.0 %reduce-scatter.7.cloned.1.call-done = bf16[1,128,2048]{2,1,0:T(8,128)(2,1)} async-done(((bf16[1,4096,2048]{2,1,0:T(8,128)(2,1)}), bf16[1,128,2048]{2,1,0:T(8,128)(2,1)}) %reduce-scatter.7.cloned.1.call-update) | async-done | bytes 524304 | tf_op jit(solution)/shard_map/reduce_scatter | solution.py:44
  483.0 1.3 convert_reduce_fusion.1
  484.6 0.5 copy-done
  485.1 1.2 fusion.79
  486.4 68.7 %all-gather.9.cloned.1.call-done = bf16[1,4096,2048]{2,1,0:T(8,128)(2,1)} async-done(((bf16[1,128,2048]{2,1,0:T(8,128)(2,1)}), bf16[1,4096,2048]{2,1,0:T(8,128)(2,1)}) %all-gather.9.cloned.1.call-update) | async-done | bytes 16777232 | tf_op jit(solution)/shard_map/all_gather | solution.py:34
  555.1 11.4 %fusion.20 = bf16[1,4096,1,192]{1,3,2,0:T(8,128)(2,1)S(1)} fusion(bf16[1,4096,2048]{2,1,0:T(8,128)(2,1)} %all-gather.9.cloned.1.call-done, bf16[2,2048,1,192]{1,3,2,0:T(8,128)(2,1)S(1)} %copy-done.8), kind=kOutput, calls=%fused_computation.29 | convolution fusion | flops 3222011904 | bytes 19136512 | tf_op jit(solution)/shard_map/bsd,dhe->bshe/dot_general | solution.py:35
  566.5 24.4 %fusion.3 = (f32[4096]{0:T(1024)S(1)}, f32[4096,4096]{0,1:T(8,128)}) fusion(bf16[1,4096,1,192]{1,3,2,0:T(8,128)(2,1)S(1)} %fusion.20), kind=kOutput, calls=%fused_computation.10 | convolution fusion | flops 2214588416 | bytes 68173824 | tf_op jit(solution)/shard_map/bqhe,bkhe->bhqk/dot_general | solution.py:20
  590.9 22.4 %fusion.1 = f32[4096]{0:T(1024)S(1)} fusion(f32[4096,4096]{0,1:T(8,128)} %get-tuple-element.18, f32[4096]{0:T(1024)S(1)} %get-tuple-element.17), kind=kLoop, calls=%fused_computation.8 | loop fusion | flops 83881984 | bytes 67141632 | tf_op jit(solution)/shard_map/reduce_sum | solution.py:24
  613.3 34.3 %convert_bitcast_fusion.1 = bf16[1,4096,2048]{2,1,0:T(8,128)(2,1)} fusion(f32[4096,4096]{0,1:T(8,128)} %get-tuple-element.18, f32[4096]{0:T(1024)S(1)} %fusion.1, f32[4096]{0:T(1024)S(1)} %get-tuple-element.17, bf16[1,4096,1,192]{1,3,2,0:T(8,128)(2,1)S(1)} %copy-done.12, bf16[2,1,64,2048]{3,2,1,0:T(8,128)(2,1)S(1)} %copy-done.10), kind=kOutput, calls=%fused_computation.22 | convolution fusion | flops 3330539520 | bytes 84705280 | tf_op jit(solution)/shard_map/bshe,hed->bsd/dot_general | solution.py:37
  647.7 105.0 %reduce-scatter.9.cloned.1.call-done = bf16[1,128,2048]{2,1,0:T(8,128)(2,1)} async-done(((bf16[1,4096,2048]{2,1,0:T(8,128)(2,1)}), bf16[1,128,2048]{2,1,0:T(8,128)(2,1)}) %reduce-scatter.9.cloned.1.call-update) | async-done | bytes 524304 | tf_op jit(solution)/shard_map/reduce_scatter | solution.py:38
  752.8 1.3 convert_reduce_fusion
  754.3 1.2 fusion.76
  755.6 68.7 %all-gather.11.cloned.1.call-done = bf16[1,4096,2048]{2,1,0:T(8,128)(2,1)} async-done(((bf16[1,128,2048]{2,1,0:T(8,128)(2,1)}), bf16[1,4096,2048]{2,1,0:T(8,128)(2,1)}) %all-gather.11.cloned.1.call-update) | async-done | bytes 16777232 | tf_op jit(solution)/shard_map/all_gather | solution.py:41
  824.3 24.5 %convert_bitcast_fusion = bf16[1,4096,2048]{2,1,0:T(8,128)(2,1)} fusion(bf16[1,4096,2048]{2,1,0:T(8,128)(2,1)} %all-gather.11.cloned.1.call-done, bf16[2,256,2048]{2,1,0:T(8,128)(2,1)S(1)} %copy-done.7, bf16[2,2048,256]{2,1,0:T(8,128)(2,1)} %param.12), kind=kOutput, calls=%fused_computation.21 | convolution fusion | flops 8607760384 | bytes 35651584 | tf_op jit(solution)/shard_map/bsf,fd->bsd/dot_general | solution.py:43
  848.9 105.1 %reduce-scatter.11.cloned.1.call-done = bf16[1,128,2048]{2,1,0:T(8,128)(2,1)} async-done(((bf16[1,4096,2048]{2,1,0:T(8,128)(2,1)}), bf16[1,128,2048]{2,1,0:T(8,128)(2,1)}) %reduce-scatter.11.cloned.1.call-update) | async-done | bytes 524304 | tf_op jit(solution)/shard_map/reduce_scatter | solution.py:44
  953.9 2.0 fusion.89
  (51 shorter events, 1.9 us)
Async XLA Ops:
  6.5 77.9 %all-gather.5.cloned.1.call-start = ((), (), s32[]{:S(2)}) async-start(), calls=%async_computation.4 | async-start | bytes 17301504 | tf_op jit(solution)/shard_map/all_gather | solution.py:34
  12.8 268.9 %reduce-scatter.5.cloned.1.call-start = ((), (), s32[]{:S(2)}) async-start(), calls=%async_computation.5 | async-start | bytes 17301504 | tf_op jit(solution)/shard_map/reduce_scatter | solution.py:38
  120.4 21.8 %copy-start.9 = (bf16[2,1,64,2048]{3,2,1,0:T(8,128)(2,1)S(1)}, bf16[2,1,64,2048]{3,2,1,0:T(8,128)(2,1)}, u32[]{:S(2)}) copy-start(bf16[2,1,64,2048]{3,2,1,0:T(8,128)(2,1)} %param.10) | copy-start | bytes 1572868
  176.5 0.7 copy-start.5
  176.5 105.2 %copy-start.2 = (bf16[1,128,2048]{2,1,0:T(8,128)(2,1)S(1)}, bf16[1,128,2048]{2,1,0:T(8,128)(2,1)}, u32[]{:S(2)}) copy-start(bf16[1,128,2048]{2,1,0:T(8,128)(2,1)} %param.7) | copy-start | bytes 1572868
  176.5 176.7 %copy-start.6 = (bf16[2,256,2048]{2,1,0:T(8,128)(2,1)S(1)}, bf16[2,256,2048]{2,1,0:T(8,128)(2,1)}, u32[]{:S(2)}) copy-start(bf16[2,256,2048]{2,1,0:T(8,128)(2,1)} %param.13) | copy-start | bytes 6291460
  176.6 176.6 %all-gather.7.cloned.1.call-start = ((), (), s32[]{:S(2)}) async-start(), calls=%async_computation.6 | async-start | bytes 17301504 | tf_op jit(solution)/shard_map/all_gather | solution.py:41
  284.5 198.5 %reduce-scatter.7.cloned.1.call-start = ((), (), s32[]{:S(2)}) async-start(), calls=%async_computation.7 | async-start | bytes 17301504 | tf_op jit(solution)/shard_map/reduce_scatter | solution.py:44
  377.9 107.2 %copy-start.4 = (f32[1,2048]{1,0:T(1,128)S(1)}, f32[1,2048]{1,0:T(1,128)}, u32[]{:S(2)}) copy-start(f32[1,2048]{1,0:T(1,128)} %get-tuple-element.13) | copy-start | bytes 24580
  377.9 177.2 %copy-start.8 = (bf16[2,2048,1,192]{1,3,2,0:T(8,128)(2,1)S(1)}, bf16[2,2048,1,192]{1,3,2,0:T(8,128)(2,1)}, u32[]{:S(2)}) copy-start(bf16[2,2048,1,192]{1,3,2,0:T(8,128)(2,1)} %param.9) | copy-start | bytes 4718596
  377.9 177.2 %all-gather.9.cloned.1.call-start = ((), (), s32[]{:S(2)}) async-start(), calls=%async_computation.8 | async-start | bytes 17301504 | tf_op jit(solution)/shard_map/all_gather | solution.py:34
  484.3 0.8 copy-start
  486.3 266.4 %reduce-scatter.9.cloned.1.call-start = ((), (), s32[]{:S(2)}) async-start(), calls=%async_computation.9 | async-start | bytes 17301504 | tf_op jit(solution)/shard_map/reduce_scatter | solution.py:38
  566.5 24.4 %copy-start.11 = (bf16[1,4096,1,192]{1,3,2,0:T(8,128)(2,1)}, bf16[1,4096,1,192]{1,3,2,0:T(8,128)(2,1)S(1)}, u32[]{:S(2)}) copy-start(bf16[1,4096,1,192]{1,3,2,0:T(8,128)(2,1)S(1)} %fusion.20) | copy-start | bytes 4718596
  590.9 22.4 %copy-start.10 = (bf16[2,1,64,2048]{3,2,1,0:T(8,128)(2,1)S(1)}, bf16[2,1,64,2048]{3,2,1,0:T(8,128)(2,1)}, u32[]{:S(2)}) copy-start(bf16[2,1,64,2048]{3,2,1,0:T(8,128)(2,1)} %param.10) | copy-start | bytes 1572868
  590.9 22.4 %copy-start.12 = (bf16[1,4096,1,192]{1,3,2,0:T(8,128)(2,1)S(1)}, bf16[1,4096,1,192]{1,3,2,0:T(8,128)(2,1)}, u32[]{:S(2)}) copy-start(bf16[1,4096,1,192]{1,3,2,0:T(8,128)(2,1)} %copy-done.11) | copy-start | bytes 4718596
  647.6 105.2 %copy-start.1 = (bf16[1,128,2048]{2,1,0:T(8,128)(2,1)S(1)}, bf16[1,128,2048]{2,1,0:T(8,128)(2,1)}, u32[]{:S(2)}) copy-start(bf16[1,128,2048]{2,1,0:T(8,128)(2,1)} %copy-done) | copy-start | bytes 1572868
  647.6 106.7 %copy-start.3 = (f32[1,2048]{1,0:T(1,128)S(1)}, f32[1,2048]{1,0:T(1,128)}, u32[]{:S(2)}) copy-start(f32[1,2048]{1,0:T(1,128)} %get-tuple-element.11) | copy-start | bytes 24580
  647.6 176.7 %copy-start.7 = (bf16[2,256,2048]{2,1,0:T(8,128)(2,1)S(1)}, bf16[2,256,2048]{2,1,0:T(8,128)(2,1)}, u32[]{:S(2)}) copy-start(bf16[2,256,2048]{2,1,0:T(8,128)(2,1)} %param.13) | copy-start | bytes 6291460
  647.7 176.6 %all-gather.11.cloned.1.call-start = ((), (), s32[]{:S(2)}) async-start(), calls=%async_computation.10 | async-start | bytes 17301504 | tf_op jit(solution)/shard_map/all_gather | solution.py:41
  755.6 198.3 %reduce-scatter.11.cloned.1.call-start = ((), (), s32[]{:S(2)}) async-start(), calls=%async_computation.11 | async-start | bytes 17301504 | tf_op jit(solution)/shard_map/reduce_scatter | solution.py:44
Sparse Core Ops, SparseCore 0:
  12.9 71.5 all-gather.4
  176.7 104.9 reduce-scatter.4
  284.6 68.5 all-gather.6
  378.1 104.8 reduce-scatter.6
  486.4 68.6 all-gather.8
  647.8 104.9 reduce-scatter.8
  755.7 68.5 all-gather.10
  849.0 104.8 reduce-scatter.10
where the time goes:
time: 968 us; the launch traced here: 963 us
  waiting for transfers between devices  697 us (72%)
  matrix products  189 us (20%)
  other arithmetic  59.1 us (6%)
  between operations  13.8 us (1%)
    reduce_scatter x4, waiting for transfers between devices, layer_stack(): reduced = lax.psum_scatter(part_sum, 'tp', scatter_dimension=1, tiled=True)  419 us
    all_gather x4, waiting for transfers between devices, layer_stack(): normed_all = lax.all_gather(normed, 'tp', axis=1, tiled=True)  278 us
    dot_general x2, matrix products, layer_stack(): jnp.einsum('bshe,hed->bsd', attended, w_out[layer_idx], preferred_element...  68.6 us
    dot_general x2, matrix products, layer_stack(): jnp.einsum('bsf,fd->bsd', hidden, w_down[layer_idx], preferred_element_ty...  49.2 us
    dot_general x2, matrix products, causal_attention(): jnp.einsum('bqhe,bkhe->bhqk', query_blk, key_blk, preferred_element_type=...  48.7 us
    reduce_sum x2, other arithmetic, causal_attention(): attn_probs = jax.nn.softmax(scores, axis=-1).astype(jnp.bfloat16)  44.2 us
    dot_general x2, matrix products, layer_stack(): jnp.einsum('bsd,dhe->bshe', normed_all, w_qkv[layer_idx], preferred_eleme...  23 us
  transfers between devices with their start and end apart: 8, of which 8 were waited for; matrix products, arithmetic and copies ran while one was open for 0% of the time, Pallas kernels for 0%

commit v1 on v0

v1 whole, which is shorter than its diff:
```python
import functools
import math

import jax
import jax.numpy as jnp
from jax import lax
from jax.experimental import pallas as pl
from jax.experimental.pallas import tpu as pltpu
from jax.sharding import PartitionSpec as P

LN_EPS = 1.0e-5
NEG_BIG = -1.0e30
MESH = pl.DeviceIdType.MESH
CORES = 2
VMEM_LIMIT = 67043328
OWN, LEFT, RIGHT, OPP = 0, 1, 2, 3
RING = 4


def layer_norm(resid_f32, ln_gain):
    row_mean = jnp.mean(resid_f32, axis=-1, keepdims=True)
    centered = resid_f32 - row_mean
    row_var = jnp.mean(centered * centered, axis=-1, keepdims=True)
    return (centered * lax.rsqrt(row_var + LN_EPS) * ln_gain).astype(jnp.bfloat16)


def dot(a, b, dims=((1,), (0,))):
    return lax.dot_general(a, b, (dims, ((), ())), preferred_element_type=jnp.float32)


class Ids:
    def __init__(self):
        self.count = 0

    def take(self, n):
        first = self.count
        self.count += n
        return first


def stack_kernel(layers, x_ref, g1_ref, g2_ref, wqt_ref, wo_ref, wu_ref, wd_ref, out_ref,
                 xg_a, xg_m, wq, wot, wu, wd, stage, qkv, keys, vals, ostage, osum, oall,
                 acc, own, psend, precv, hop, comb, direct, hid, res,
                 send_sem, recv_sem, local_sem, ids):
    rows, width = res.shape
    half = rows // 2
    me = lax.axis_index("tp")
    core = lax.rem(me, CORES)
    other = 1 - core
    xpos = lax.rem(lax.div(me, CORES), RING)
    ypos = lax.div(me, CORES * RING)

    def dev(y, x, c):
        return (lax.rem(y, RING) * RING + lax.rem(x, RING)) * CORES + c

    partner = dev(ypos, xpos, other)
    xdev = {LEFT: dev(ypos, xpos + 3, core), RIGHT: dev(ypos, xpos + 1, core), OPP: dev(ypos, xpos + 2, core)}
    ydev = {LEFT: dev(ypos + 3, xpos, core), RIGHT: dev(ypos + 1, xpos, core)}

    pending, pending_weights = [], []

    def send(k, src, dst, device, queue=pending):
        copy = pltpu.make_async_remote_copy(src_ref=src, dst_ref=dst, send_sem=send_sem.at[k], recv_sem=recv_sem.at[k],
                                            device_id={"tp": device}, device_id_type=MESH)
        copy.start()
        queue.append(copy)

    def arrived(k, dst):
        pltpu.make_async_remote_copy(src_ref=dst, dst_ref=dst, send_sem=send_sem.at[k], recv_sem=recv_sem.at[k],
                                     device_id={"tp": partner}, device_id_type=MESH).wait_recv()

    def drain(queue=pending):
        for copy in queue:
            copy.wait_send()
        queue.clear()

    class Gather:
        def __init__(self, buf, ring):
            self.buf, self.ring, self.k = buf, ring, ids.take(12)
            self.a, self.b = pl.ds(0, half), pl.ds(half, half)

        def start(self):
            own_rows = self.buf.at[OWN, core]
            right, left = self.ring[RIGHT], self.ring[LEFT]
            send(self.k, own_rows.at[self.a], self.buf.at[LEFT, core, self.a], right)
            send(self.k + 1, own_rows.at[self.b], self.buf.at[RIGHT, core, self.b], left)
            send(self.k + 2, own_rows, self.buf.at[OWN, core], partner)
            send(self.k + 3, own_rows.at[self.b], self.buf.at[LEFT, core, self.b], right)
            send(self.k + 4, own_rows.at[self.a], self.buf.at[RIGHT, core, self.a], left)

        def relay(self):
            arrived(self.k, self.buf.at[LEFT, core, self.a])
            send(self.k + 5, self.buf.at[LEFT, core, self.a], self.buf.at[OPP, core, self.a], self.ring[RIGHT])
            arrived(self.k + 1, self.buf.at[RIGHT, core, self.b])
            send(self.k + 6, self.buf.at[RIGHT, core, self.b], self.buf.at[OPP, core, self.b], self.ring[LEFT])

        def near(self):
            arrived(self.k + 3, self.buf.at[LEFT, core, self.b])
            send(self.k + 7, self.buf.at[LEFT, core], self.buf.at[LEFT, core], partner)
            arrived(self.k + 4, self.buf.at[RIGHT, core, self.a])
            send(self.k + 8, self.buf.at[RIGHT, core], self.buf.at[RIGHT, core], partner)

        def far(self):
            arrived(self.k + 5, self.buf.at[OPP, core, self.a])
            arrived(self.k + 6, self.buf.at[OPP, core, self.b])
            send(self.k + 9, self.buf.at[OPP, core], self.buf.at[OPP, core], partner)

        def wait(self, slot):
            arrived(self.k + {OWN: 2, LEFT: 7, RIGHT: 8, OPP: 9}[slot], self.buf.at[slot, other])

    class Weights:
        def __init__(self, src, buf, ring):
            self.src, self.buf, self.ring = src, buf, ring
            self.k = ids.take(6)
            n = buf.shape[1] // 2
            self.a, self.b = pl.ds(0, n), pl.ds(n, n)

        def local(self, sem):
            copy = pltpu.make_async_copy(self.src, self.buf.at[OWN], local_sem.at[sem])
            copy.start()
            return copy

        def start(self):
            right, left = self.ring[RIGHT], self.ring[LEFT]
            send(self.k, self.src.at[self.a], self.buf.at[LEFT, self.a], right, pending_weights)
            send(self.k + 1, self.src.at[self.b], self.buf.at[RIGHT, self.b], left, pending_weights)
            send(self.k + 2, self.src.at[self.b], self.buf.at[LEFT, self.b], right, pending_weights)
            send(self.k + 3, self.src.at[self.a], self.buf.at[RIGHT, self.a], left, pending_weights)

        def relay(self):
            arrived(self.k, self.buf.at[LEFT, self.a])
            send(self.k + 4, self.buf.at[LEFT, self.a], self.buf.at[OPP, self.a], self.ring[RIGHT], pending_weights)
            arrived(self.k + 1, self.buf.at[RIGHT, self.b])
            send(self.k + 5, self.buf.at[RIGHT, self.b], self.buf.at[OPP, self.b], self.ring[LEFT], pending_weights)

        def wait_near(self):
            arrived(self.k + 2, self.buf.at[LEFT, self.b])
            arrived(self.k + 3, self.buf.at[RIGHT, self.a])

        def wait_far(self):
            arrived(self.k + 4, self.buf.at[OPP, self.a])
            arrived(self.k + 5, self.buf.at[OPP, self.b])

    class Reduce:
        def __init__(self, ring):
            self.ring, self.k = ring, ids.take(10)
            self.a, self.b = pl.ds(0, half), pl.ds(half, half)

        def give(self, slot):
            own[slot] = acc[core]
            psend[slot] = acc[other].astype(jnp.bfloat16)
            send(self.k + slot, psend.at[slot], precv.at[slot], partner)

        def pair(self, slot):
            arrived(self.k + slot, precv.at[slot])

        def term(self, slot, part):
            return own[slot, part, :] + precv[slot, part, :].astype(jnp.float32)

        def far(self):
            self.pair(OPP)
            comb[0] = self.term(OPP, self.a).astype(jnp.bfloat16)
            send(self.k + 4, comb.at[0], hop.at[0], self.ring[RIGHT])
            comb[1] = self.term(OPP, self.b).astype(jnp.bfloat16)
            send(self.k + 5, comb.at[1], hop.at[1], self.ring[LEFT])

        def near(self, slot):
            self.pair(slot)
            if slot == RIGHT:
                comb[2] = self.term(RIGHT, self.b).astype(jnp.bfloat16)
                send(self.k + 6, comb.at[2], direct.at[0, 1], self.ring[RIGHT])
            else:
                comb[3] = self.term(LEFT, self.a).astype(jnp.bfloat16)
                send(self.k + 7, comb.at[3], direct.at[1, 0], self.ring[LEFT])

        def relay(self):
            arrived(self.k + 4, hop.at[0])
            comb[4] = (self.term(RIGHT, self.a) + hop[0].astype(jnp.float32)).astype(jnp.bfloat16)
            send(self.k + 8, comb.at[4], direct.at[0, 0], self.ring[RIGHT])
            arrived(self.k + 5, hop.at[1])
            comb[5] = (self.term(LEFT, self.b) + hop[1].astype(jnp.float32)).astype(jnp.bfloat16)
            send(self.k + 9, comb.at[5], direct.at[1, 1], self.ring[LEFT])

        def finish(self):
            self.pair(OWN)
            arrived(self.k + 6, direct.at[0, 1])
            arrived(self.k + 7, direct.at[1, 0])
            arrived(self.k + 8, direct.at[0, 0])
            arrived(self.k + 9, direct.at[1, 1])
            for i, part in enumerate((self.a, self.b)):
                total = self.term(OWN, part) + direct[0, i].astype(jnp.float32) + direct[1, i].astype(jnp.float32)
                res[part, :] = (res[part, :].astype(jnp.float32) + total).astype(jnp.bfloat16)

    w_q = [Weights(wqt_ref.at[l], wq.at[l], xdev) for l in range(layers)]
    w_o = [Weights(wo_ref.at[l], wot.at[l], xdev) for l in range(layers)]
    w_u = [Weights(wu_ref.at[l], wu.at[l], ydev) for l in range(layers)]
    w_d = [Weights(wd_ref.at[l], wd.at[l], ydev) for l in range(layers)]
    everything = [w for l in range(layers) for w in (w_q[l], w_o[l], w_u[l], w_d[l])]
    copies = [w.local(i) for i, w in enumerate(everything)]

    barrier = pltpu.get_barrier_semaphore()
    peers = [partner, *xdev.values(), *ydev.values()]
    for peer in peers:
        pl.semaphore_signal(barrier, inc=1, device_id={"tp": peer}, device_id_type=MESH)
    res[...] = x_ref[...]
    pl.semaphore_wait(barrier, len(peers))

    head_dim = keys.shape[1]
    block = qkv.shape[2]
    column = RING * block

    def attention_front(l, gather):
        k = ids.take(3 * RING)
        slots = {LEFT: RIGHT, RIGHT: LEFT, OPP: OPP}
        order = (OWN, LEFT, RIGHT, OPP)

        def heads(s, slot):
            rows_in = xg_a[s].reshape(CORES * rows, width)
            part = dot(wq[l, slot], rows_in, ((1,), (1,))).astype(jnp.bfloat16)
            shift = {OWN: 0, LEFT: 3, RIGHT: 1, OPP: 2}[s]
            g = lax.rem(ypos + shift, RING) * RING + xpos
            if slot == OWN:
                qkv[g] = part
            else:
                stage[s, slot - 1] = part
                send(k + 3 * s + slot - 1, stage.at[s, slot - 1], qkv.at[g], xdev[slot])

        def receive():
            for s in order:
                shift = {OWN: 0, LEFT: 3, RIGHT: 1, OPP: 2}[s]
                for slot in (LEFT, RIGHT, OPP):
                    x_from = {LEFT: xpos + 1, RIGHT: xpos + 3, OPP: xpos + 2}[slot]
                    g = lax.rem(ypos + shift, RING) * RING + lax.rem(x_from, RING)
                    arrived(k + 3 * s + slot - 1, qkv.at[g])

        return heads, receive

    def prepare_keys():
        def body(g, carry):
            keys[pl.ds(pl.multiple_of(g * block, block), block), :] = (
                qkv[g, head_dim:2 * head_dim, :].astype(jnp.float32).T.astype(jnp.bfloat16))
            vals[g // RING, :, pl.ds(pl.multiple_of(lax.rem(g, RING) * block, block), block)] = qkv[g, 2 * head_dim:, :]
            return carry

        lax.fori_loop(0, RING * RING, body, 0)

    def attend(shift):
        y = lax.rem(ypos + shift, RING)

        def one_block(x, carry):
            g = y * RING + x
            query = (qkv[g, :head_dim, :].astype(jnp.float32) * head_dim ** -0.5).astype(jnp.bfloat16)

            def scores(chunk):
                return dot(keys[pl.ds(pl.multiple_of(chunk * column, column), column), :], query)

            s = scores(y)
            key_pos = lax.broadcasted_iota(jnp.int32, s.shape, 0)
            query_pos = lax.broadcasted_iota(jnp.int32, s.shape, 1) + x * block
            s = jnp.where(query_pos >= key_pos, s, NEG_BIG)
            top = jnp.max(s, axis=0, keepdims=True)
            p = jnp.exp(s - top)
            total = jnp.sum(p, axis=0, keepdims=True)
            osum[...] = dot(vals[y], p.astype(jnp.bfloat16))

            def more(chunk, state):
                top, total = state
                s = scores(chunk)
                new_top = jnp.maximum(top, jnp.max(s, axis=0, keepdims=True))
                scale = jnp.exp(top - new_top)
                p = jnp.exp(s - new_top)
                total = total * scale + jnp.sum(p, axis=0, keepdims=True)
                osum[...] = osum[...] * scale + dot(vals[chunk], p.astype(jnp.bfloat16))
                return new_top, total

            top, total = lax.fori_loop(0, y, more, (top, total))
            ostage[shift, x] = (osum[...] / total).astype(jnp.bfloat16)
            return carry

        lax.fori_loop(0, RING, one_block, 0)

    def exchange_o(shift, k):
        oall[shift, OWN] = ostage[shift, xpos]
        for slot, x_to in ((LEFT, xpos + 1), (RIGHT, xpos + 3), (OPP, xpos + 2)):
            to = {LEFT: xdev[RIGHT], RIGHT: xdev[LEFT], OPP: xdev[OPP]}[slot]
            send(k + slot - 1, ostage.at[shift, lax.rem(x_to, RING)], oall.at[shift, slot], to)

    def project(l, shift, slot, k, reduce):
        for source in (LEFT, RIGHT, OPP):
            arrived(k + source - 1, oall.at[shift, source])
        o_all = oall[shift].reshape(RING * head_dim, block)
        w_all = wot[l].reshape(RING * head_dim, width)
        acc[...] = dot(o_all, w_all, ((0,), (0,))).reshape(acc.shape)
        reduce.give(slot)

    def mlp_slot(l, s, reduce):
        def up(j, carry):
            rows_in = xg_m[s].reshape(CORES * rows, width)
            h = jax.nn.gelu(dot(rows_in, wu[l, j]), approximate=True).astype(jnp.bfloat16)
            hid[:, pl.ds(pl.multiple_of(j * wu.shape[3], wu.shape[3]), wu.shape[3])] = h
            return carry

        lax.fori_loop(0, RING, up, 0)
        tile = 512

        def down(j, carry):
            cols = pl.ds(pl.multiple_of(j * tile, tile), tile)
            w_all = wd[l, :, :, cols].reshape(hid.shape[1], tile)
            acc[:, :, cols] = dot(hid[...], w_all).reshape(CORES, rows, tile)
            return carry

        lax.fori_loop(0, width // tile, down, 0)
        reduce.give(s)

    for l in range(layers):
        drain()
        gather = Gather(xg_a, ydev)
        xg_a[OWN, core] = layer_norm(res[...].astype(jnp.float32), g1_ref[l, :][None, :])
        gather.start()
        if l == 0:
            w_q[0].start()
            w_o[0].start()
        gather.relay()
        gather.near()
        if l == 0:
            w_q[0].relay()
            w_o[0].relay()
        gather.far()
        if l == 0:
            w_u[0].start()
            w_d[0].start()
            for i in range(2):
                copies[i].wait()
        w_q[l].wait_near()
        heads, receive = attention_front(l, gather)
        for s in (OWN, LEFT, RIGHT, OPP):
            gather.wait(s)
            if s == OWN:
                w_q[l].wait_far()
            for slot in (LEFT, RIGHT, OPP, OWN):
                heads(s, slot)
        if l == 0:
            w_u[0].relay()
        receive()
        prepare_keys()
        if l + 1 < layers:
            w_q[l + 1].start()
            w_o[l + 1].start()
        k_o = ids.take(3 * RING)
        reduce = Reduce(ydev)
        order = ((2, OPP), (3, LEFT), (1, RIGHT), (0, OWN))

        def finish_segment(i):
            shift, slot = order[i]
            project(l, shift, slot, k_o + 3 * shift, reduce)

        w_o[l].wait_near()
        w_o[l].wait_far()
        for i, (shift, slot) in enumerate(order):
            attend(shift)
            exchange_o(shift, k_o + 3 * shift)
            if i == 1:
                finish_segment(0)
            if i == 2:
                reduce.far()
                finish_segment(1)
                if l == 0:
                    w_d[0].relay()
                if l + 1 < layers:
                    w_q[l + 1].relay()
            if i == 3:
                reduce.near(LEFT)
                finish_segment(2)
        reduce.near(RIGHT)
        finish_segment(3)
        reduce.relay()
        reduce.finish()
        if l + 1 < layers:
            w_o[l + 1].relay()
        drain()

        gather = Gather(xg_m, xdev)
        xg_m[OWN, core] = layer_norm(res[...].astype(jnp.float32), g2_ref[l, :][None, :])
        gather.start()
        if l + 1 < layers:
            w_u[l + 1].start()
            w_d[l + 1].start()
        if l == 0:
            for i in range(2, len(copies)):
                copies[i].wait()
        reduce = Reduce(xdev)
        gather.relay()
        w_u[l].wait_near()
        w_d[l].wait_near()
        w_u[l].wait_far()
        w_d[l].wait_far()
        gather.wait(OWN)
        mlp_slot(l, OWN, reduce)
        gather.near()
        gather.wait(LEFT)
        mlp_slot(l, LEFT, reduce)
        reduce.near(LEFT)
        gather.far()
        gather.wait(RIGHT)
        mlp_slot(l, RIGHT, reduce)
        reduce.near(RIGHT)
        gather.wait(OPP)
        mlp_slot(l, OPP, reduce)
        reduce.far()
        if l + 1 < layers:
            w_u[l + 1].relay()
        reduce.relay()
        if l + 1 < layers:
            w_d[l + 1].relay()
        reduce.finish()
    drain()
    drain(pending_weights)
    out_ref[...] = res[...]


def solution(mesh):
    def layer_stack(x_local, ln1_gain, w_qkv, w_out, ln2_gain, w_up, w_down):
        batch, rows, width = x_local.shape
        layers, _, _, three_e = w_qkv.shape
        head_dim = three_e // 3
        ff = w_up.shape[2]
        block = CORES * rows
        wqt = w_qkv.reshape(layers, width, three_e).transpose(0, 2, 1)
        wo = w_out.reshape(layers, head_dim, width)
        bf16, f32 = jnp.bfloat16, jnp.float32
        vmem = pltpu.VMEM
        n_ids = 200
        hbm = pl.BlockSpec(memory_space=pltpu.HBM)
        in_vmem = pl.BlockSpec(memory_space=pltpu.VMEM)
        scratch = [
            vmem((RING, CORES, rows, width), bf16),
            vmem((RING, CORES, rows, width), bf16),
            vmem((layers, RING, three_e, width), bf16),
            vmem((layers, RING, head_dim, width), bf16),
            vmem((layers, RING, width, ff), bf16),
            vmem((layers, RING, ff, width), bf16),
            vmem((RING, RING - 1, three_e, block), bf16),
            vmem((RING * RING, three_e, block), bf16),
            vmem((RING * RING * block, head_dim), bf16),
            vmem((RING, head_dim, RING * block), bf16),
            vmem((RING, RING, head_dim, block), bf16),
            vmem((head_dim, block), f32),
            vmem((RING, RING, head_dim, block), bf16),
            vmem((CORES, rows, width), f32),
            vmem((RING, rows, width), f32),
            vmem((RING, rows, width), bf16),
            vmem((RING, rows, width), bf16),
            vmem((2, rows // 2, width), bf16),
            vmem((6, rows // 2, width), bf16),
            vmem((2, 2, rows // 2, width), bf16),
            vmem((block, RING * ff), bf16),
            vmem((rows, width), bf16),
            pltpu.SemaphoreType.DMA((n_ids,)),
            pltpu.SemaphoreType.DMA((n_ids,)),
            pltpu.SemaphoreType.DMA((4 * layers,)),
        ]

        def kernel(*refs):
            ids = Ids()
            stack_kernel(layers, *refs, ids)
            assert ids.count <= n_ids, ids.count

        out = pl.pallas_call(
            kernel,
            out_shape=jax.ShapeDtypeStruct((rows, width), bf16),
            in_specs=[in_vmem, in_vmem, in_vmem, hbm, hbm, hbm, hbm],
            out_specs=in_vmem,
            scratch_shapes=scratch,
            compiler_params=pltpu.CompilerParams(collective_id=0, has_side_effects=True, vmem_limit_bytes=VMEM_LIMIT),
        )(x_local.reshape(rows, width), ln1_gain, ln2_gain, wqt, wo, w_up, w_down)
        return out.reshape(batch, rows, width)

    return jax.shard_map(layer_stack, mesh=mesh, in_specs=(P('dp', 'tp', None), P(), P(None, None, 'tp', None), P(None, 'tp', None, None), P(), P(None, None, 'tp'), P(None, 'tp', None)), out_specs=P('dp', 'tp', None), check_vma=False)
```

time: 968 us -> 339 us (0.35)
  waiting for transfers between devices: 697 us -> 0 us
  Pallas kernels: 0 us -> 332 us
  matrix products: 189 us -> 0 us
  other arithmetic: 59.1 us -> 0 us
  between operations: 13.8 us -> 0.2 us
    reduce_scatter x4 -> x0, waiting for transfers between devices: 419 us -> none  [layer_stack(): reduced = lax.psum_scatter(part_sum, 'tp', scatter_dimension=1, tiled=True)]
    pallas_call x0 -> x1, Pallas kernels: none -> 332 us  [layer_stack(): pl.pallas_call(kernel, out_shape=jax.ShapeDtypeStruct((rows, width), bf16...]
    all_gather x4 -> x0, waiting for transfers between devices: 278 us -> none  [layer_stack(): normed_all = lax.all_gather(normed, 'tp', axis=1, tiled=True)]
    dot_general x8 -> x0, matrix products: 189 us -> none  [the longest x2 68.6 us: layer_stack(): jnp.einsum('bshe,hed->bsd', attended, w_out[layer_idx], preferred_element...]
    reduce_sum x10 -> x0, other arithmetic: 51.4 us -> none  [the longest x2 44.2 us: causal_attention(): attn_probs = jax.nn.softmax(scores, axis=-1).astype(jnp.bfloat16)]
  transfers between devices with their start and end apart: 8 -> 0, of which waited for: 8 -> 0; matrix products, arithmetic and copies ran while one was open for 0% -> 0% of each run, Pallas kernels for 0% -> 0%
where the time goes in v1:
time: 339 us; the launch traced here: 334 us
  Pallas kernels  332 us (98%)
    pallas_call x1, Pallas kernels, layer_stack(): pl.pallas_call(kernel, out_shape=jax.ShapeDtypeStruct((rows, width), bf16...  332 us

profile of v1, /device:TPU:97, one launch (start us, length us, event | category | flops | bytes accessed | tf_op | source)
XLA Modules:
  0.0 334.0 jit_solution(17171585305629729956)
XLA Ops:
  0.0 331.9 %shard_map.73 = bf16[128,2048]{1,0:T(8,128)(2,1)} custom-call(bf16[128,2048]{1,0:T(8,128)(2,1)} %bitcast.8, f32[2,2048]{1,0:T(2,128)} %refs_1_.1, f32[2,2048]{1,0:T(2,128)} %refs_2_.1, bf16[2,192,2048]{2,1,0:T(8,128)(2,1)} %bitcast.7, bf16[2,64,2048]{2,1,0:T(8,128)(2,1)} %bitcast.9, bf16[2,2048,256]{2,1,0:T(8,128)(2,1)} %refs_5_.1, bf16[2,256,2048]{2,1,0:T(8,128)(2,1)} %refs_6_.1), custom_call_target="tpu_custom_call" | custom-call | tf_op jit(solution)/shard_map/pallas_call | solution.py:468
  331.9 1.9 copy.9

commit v2 on v1

v2 whole, which is shorter than its diff:
```python
import functools
import math

import jax
import jax.numpy as jnp
from jax import lax
from jax.experimental import pallas as pl
from jax.experimental.pallas import tpu as pltpu
from jax.sharding import PartitionSpec as P

LN_EPS = 1.0e-5
NEG_BIG = -1.0e30
MESH = pl.DeviceIdType.MESH
CORES = 2
VMEM_LIMIT = 67043328
OWN, LEFT, RIGHT, OPP = 0, 1, 2, 3
RING = 4


def layer_norm(resid_f32, ln_gain):
    row_mean = jnp.mean(resid_f32, axis=-1, keepdims=True)
    centered = resid_f32 - row_mean
    row_var = jnp.mean(centered * centered, axis=-1, keepdims=True)
    return (centered * lax.rsqrt(row_var + LN_EPS) * ln_gain).astype(jnp.bfloat16)


def dot(a, b, dims=((1,), (0,))):
    return lax.dot_general(a, b, (dims, ((), ())), preferred_element_type=jnp.float32)


class Ids:
    def __init__(self):
        self.count = 0

    def take(self, n):
        first = self.count
        self.count += n
        return first


def stack_kernel(layers, x_ref, g1_ref, g2_ref, wqt_ref, wo_ref, wu_ref, wd_ref, out_ref,
                 xg_a, xg_m, wq, wot, wu, wd, stage, qkv, keys, vals, ostage, score, osum, oall,
                 own, psend, precv, hop, comb, direct, hid, res,
                 send_sem, recv_sem, local_sem, ids):
    rows, width = res.shape
    half = rows // 2
    me = lax.axis_index("tp")
    part = lax.axis_index("dp") + 0 * me
    core = lax.rem(me, CORES)
    other = 1 - core
    xpos = lax.rem(lax.div(me, CORES), RING)
    ypos = lax.div(me, CORES * RING)

    def dev(y, x, c):
        return (lax.rem(y, RING) * RING + lax.rem(x, RING)) * CORES + c

    partner = dev(ypos, xpos, other)
    xdev = {LEFT: dev(ypos, xpos + 3, core), RIGHT: dev(ypos, xpos + 1, core), OPP: dev(ypos, xpos + 2, core)}
    ydev = {LEFT: dev(ypos + 3, xpos, core), RIGHT: dev(ypos + 1, xpos, core)}

    pending, pending_weights = {}, {}

    def send(k, src, dst, device, queue=pending):
        copy = pltpu.make_async_remote_copy(src_ref=src(), dst_ref=dst, send_sem=send_sem.at[k], recv_sem=recv_sem.at[k],
                                            device_id={"dp": part, "tp": device}, device_id_type=MESH)
        copy.start()
        if queue is not None:
            queue[k] = src

    def arrived(k, dst):
        pltpu.make_async_remote_copy(src_ref=dst, dst_ref=dst, send_sem=send_sem.at[k], recv_sem=recv_sem.at[k],
                                     device_id={"dp": part, "tp": partner}, device_id_type=MESH).wait_recv()

    def drain(queue=pending):
        for k, src in queue.items():
            pltpu.make_async_remote_copy(src_ref=src(), dst_ref=src(), send_sem=send_sem.at[k], recv_sem=recv_sem.at[k],
                                         device_id={"dp": part, "tp": partner}, device_id_type=MESH).wait_send()
        queue.clear()

    class Gather:
        def __init__(self, buf, ring):
            self.buf, self.ring, self.k = buf, ring, ids.take(12)
            self.a, self.b = pl.ds(0, half), pl.ds(half, half)

        def start(self):
            own_rows = self.buf.at[OWN, core]
            right, left = self.ring[RIGHT], self.ring[LEFT]
            send(self.k, lambda: own_rows.at[self.a], self.buf.at[LEFT, core, self.a], right)
            send(self.k + 1, lambda: own_rows.at[self.b], self.buf.at[RIGHT, core, self.b], left)
            send(self.k + 2, lambda: own_rows, self.buf.at[OWN, core], partner)
            send(self.k + 3, lambda: own_rows.at[self.b], self.buf.at[LEFT, core, self.b], right)
            send(self.k + 4, lambda: own_rows.at[self.a], self.buf.at[RIGHT, core, self.a], left)

        def relay(self):
            arrived(self.k, self.buf.at[LEFT, core, self.a])
            send(self.k + 5, lambda: self.buf.at[LEFT, core, self.a], self.buf.at[OPP, core, self.a], self.ring[RIGHT])
            arrived(self.k + 1, self.buf.at[RIGHT, core, self.b])
            send(self.k + 6, lambda: self.buf.at[RIGHT, core, self.b], self.buf.at[OPP, core, self.b], self.ring[LEFT])

        def near(self):
            arrived(self.k + 3, self.buf.at[LEFT, core, self.b])
            send(self.k + 7, lambda: self.buf.at[LEFT, core], self.buf.at[LEFT, core], partner)
            arrived(self.k + 4, self.buf.at[RIGHT, core, self.a])
            send(self.k + 8, lambda: self.buf.at[RIGHT, core], self.buf.at[RIGHT, core], partner)

        def far(self):
            arrived(self.k + 5, self.buf.at[OPP, core, self.a])
            arrived(self.k + 6, self.buf.at[OPP, core, self.b])
            send(self.k + 9, lambda: self.buf.at[OPP, core], self.buf.at[OPP, core], partner)

        def wait(self, slot):
            arrived(self.k + {OWN: 2, LEFT: 7, RIGHT: 8, OPP: 9}[slot], self.buf.at[slot, other])

    class Weights:
        def __init__(self, src, buf, ring):
            self.src, self.buf, self.ring = src, buf, ring
            self.k = ids.take(6)
            n = buf.shape[1] // 2
            self.a, self.b = pl.ds(0, n), pl.ds(n, n)

        def local(self, sem):
            copy = pltpu.make_async_copy(self.src, self.buf.at[OWN], local_sem.at[sem])
            copy.start()
            return copy

        def start(self):
            right, left = self.ring[RIGHT], self.ring[LEFT]
            send(self.k, lambda: self.src.at[self.a], self.buf.at[LEFT, self.a], right, pending_weights)
            send(self.k + 1, lambda: self.src.at[self.b], self.buf.at[RIGHT, self.b], left, pending_weights)

        def start_rest(self):
            right, left = self.ring[RIGHT], self.ring[LEFT]
            send(self.k + 2, lambda: self.src.at[self.b], self.buf.at[LEFT, self.b], right, pending_weights)
            send(self.k + 3, lambda: self.src.at[self.a], self.buf.at[RIGHT, self.a], left, pending_weights)

        def relay(self):
            arrived(self.k, self.buf.at[LEFT, self.a])
            send(self.k + 4, lambda: self.buf.at[LEFT, self.a], self.buf.at[OPP, self.a], self.ring[RIGHT], pending_weights)
            arrived(self.k + 1, self.buf.at[RIGHT, self.b])
            send(self.k + 5, lambda: self.buf.at[RIGHT, self.b], self.buf.at[OPP, self.b], self.ring[LEFT], pending_weights)

        def wait_near(self):
            arrived(self.k + 2, self.buf.at[LEFT, self.b])
            arrived(self.k + 3, self.buf.at[RIGHT, self.a])

        def wait_far(self):
            arrived(self.k + 4, self.buf.at[OPP, self.a])
            arrived(self.k + 5, self.buf.at[OPP, self.b])

    class Reduce:
        def __init__(self, ring):
            self.ring, self.k = ring, ids.take(10)
            self.a, self.b = pl.ds(0, half), pl.ds(half, half)

        def put(self, slot, cols, term):
            first, second = term[:rows], term[rows:]
            own[slot, :, cols] = jnp.where(core == 0, first, second)
            psend[slot, :, cols] = jnp.where(core == 0, second, first).astype(jnp.bfloat16)

        def give(self, slot):
            send(self.k + slot, lambda: psend.at[slot], precv.at[slot], partner)

        def pair(self, slot):
            arrived(self.k + slot, precv.at[slot])

        def term(self, slot, part):
            return own[slot, part, :] + precv[slot, part, :].astype(jnp.float32)

        def far(self):
            self.pair(OPP)
            comb[0] = self.term(OPP, self.a).astype(jnp.bfloat16)
            send(self.k + 4, lambda: comb.at[0], hop.at[0], self.ring[RIGHT])
            comb[1] = self.term(OPP, self.b).astype(jnp.bfloat16)
            send(self.k + 5, lambda: comb.at[1], hop.at[1], self.ring[LEFT])

        def near(self, slot):
            self.pair(slot)
            if slot == RIGHT:
                comb[2] = self.term(RIGHT, self.b).astype(jnp.bfloat16)
                send(self.k + 6, lambda: comb.at[2], direct.at[0, 1], self.ring[RIGHT])
            else:
                comb[3] = self.term(LEFT, self.a).astype(jnp.bfloat16)
                send(self.k + 7, lambda: comb.at[3], direct.at[1, 0], self.ring[LEFT])

        def relay(self):
            arrived(self.k + 4, hop.at[0])
            comb[4] = (self.term(RIGHT, self.a) + hop[0].astype(jnp.float32)).astype(jnp.bfloat16)
            send(self.k + 8, lambda: comb.at[4], direct.at[0, 0], self.ring[RIGHT])
            arrived(self.k + 5, hop.at[1])
            comb[5] = (self.term(LEFT, self.b) + hop[1].astype(jnp.float32)).astype(jnp.bfloat16)
            send(self.k + 9, lambda: comb.at[5], direct.at[1, 1], self.ring[LEFT])

        def finish(self):
            self.pair(OWN)
            arrived(self.k + 6, direct.at[0, 1])
            arrived(self.k + 7, direct.at[1, 0])
            arrived(self.k + 8, direct.at[0, 0])
            arrived(self.k + 9, direct.at[1, 1])
            for i, part in enumerate((self.a, self.b)):
                total = self.term(OWN, part) + direct[0, i].astype(jnp.float32) + direct[1, i].astype(jnp.float32)
                res[part, :] = (res[part, :].astype(jnp.float32) + total).astype(jnp.bfloat16)

    w_q = [Weights(wqt_ref.at[l], wq.at[l], xdev) for l in range(layers)]
    w_o = [Weights(wo_ref.at[l], wot.at[l], xdev) for l in range(layers)]
    w_u = [Weights(wu_ref.at[l], wu.at[l], ydev) for l in range(layers)]
    w_d = [Weights(wd_ref.at[l], wd.at[l], ydev) for l in range(layers)]
    everything = [w for l in range(layers) for w in (w_q[l], w_o[l], w_u[l], w_d[l])]
    copies = [w.local(i) for i, w in enumerate(everything)]

    barrier = pltpu.get_barrier_semaphore()
    peers = [partner, *xdev.values(), *ydev.values()]
    for peer in peers:
        pl.semaphore_signal(barrier, inc=1, device_id={"dp": part, "tp": peer}, device_id_type=MESH)
    res[...] = x_ref[...]
    pl.semaphore_wait(barrier, len(peers))

    head_dim = keys.shape[1]
    block = qkv.shape[2]
    column = RING * block

    def attention_front(l, gather):
        k = ids.take(3 * RING)
        order = (OWN, LEFT, RIGHT, OPP)

        def heads(s, slots):
            rows_in = xg_a[s].reshape(CORES * rows, width)
            n = len(slots)
            weights = wq[l, slots[0]:slots[0] + n].reshape(n * wq.shape[2], width)
            part = dot(weights, rows_in, ((1,), (1,))).astype(jnp.bfloat16).reshape(n, wq.shape[2], block)
            shift = {OWN: 0, LEFT: 3, RIGHT: 1, OPP: 2}[s]
            g = lax.rem(ypos + shift, RING) * RING + xpos
            for i, slot in enumerate(slots):
                if slot == OWN:
                    qkv[g] = part[i]
                else:
                    stage[s, slot - 1] = part[i]
                    send(k + 3 * s + slot - 1, lambda slot=slot: stage.at[s, slot - 1], qkv.at[g], xdev[slot])

        def receive():
            for s in order:
                shift = {OWN: 0, LEFT: 3, RIGHT: 1, OPP: 2}[s]
                for slot in (LEFT, RIGHT, OPP):
                    x_from = {LEFT: xpos + 1, RIGHT: xpos + 3, OPP: xpos + 2}[slot]
                    g = lax.rem(ypos + shift, RING) * RING + lax.rem(x_from, RING)
                    arrived(k + 3 * s + slot - 1, qkv.at[g])

        return heads, receive

    def prepare_keys():
        def body(g, carry):
            keys[pl.ds(pl.multiple_of(g * block, block), block), :] = (
                qkv[g, head_dim:2 * head_dim, :].astype(jnp.float32).T.astype(jnp.bfloat16))
            vals[g // RING, :, pl.ds(pl.multiple_of(lax.rem(g, RING) * block, block), block)] = qkv[g, 2 * head_dim:, :]
            return carry

        lax.fori_loop(0, RING * RING, body, 0)

    def attend(shift, i):
        y = lax.rem(ypos + shift, RING)
        queries = [(qkv[y * RING + x, :head_dim, :].astype(jnp.float32) * head_dim ** -0.5).astype(jnp.bfloat16)
                   for x in range(RING)]

        def step(chunk, state):
            k_all = keys[pl.ds(pl.multiple_of(chunk * column, column), column), :]
            v_all = vals[chunk]
            diagonal = state is None
            tops, new = [], []
            for x in range(RING):
                n = (x + 1) * block if diagonal else column
                s = dot(k_all[:n], queries[x])
                if diagonal:
                    key_pos = lax.broadcasted_iota(jnp.int32, (block, block), 0)
                    query_pos = lax.broadcasted_iota(jnp.int32, (block, block), 1)
                    last = jnp.where(query_pos >= key_pos, s[n - block:], NEG_BIG)
                    score[x, n - block:n, :] = last
                    top = jnp.max(last, axis=0, keepdims=True)
                    if x:
                        score[x, :n - block, :] = s[:n - block]
                        top = jnp.maximum(top, jnp.max(s[:n - block], axis=0, keepdims=True))
                else:
                    score[x] = s
                    top = jnp.max(s, axis=0, keepdims=True)
                tops.append(top)
            for x in range(RING):
                n = (x + 1) * block if diagonal else column
                top = tops[x] if diagonal else jnp.maximum(state[2 * x], tops[x])
                p = jnp.exp(score[x, :n, :] - top)
                total = jnp.sum(p, axis=0, keepdims=True)
                weighted = dot(v_all[:, :n], p.astype(jnp.bfloat16))
                if not diagonal:
                    scale = jnp.exp(state[2 * x] - top)
                    weighted = osum[x] * scale + weighted
                    total = state[2 * x + 1] * scale + total
                osum[x] = weighted
                new += [top, total]
            return tuple(new)

        state = lax.fori_loop(0, y, step, step(y, None))
        for x in range(RING):
            ostage[i, x] = (osum[x] / state[2 * x + 1]).astype(jnp.bfloat16)

    def exchange_o(i, k):
        oall[i, OWN] = ostage[i, xpos]
        for slot, x_to in ((LEFT, xpos + 1), (RIGHT, xpos + 3), (OPP, xpos + 2)):
            to = {LEFT: xdev[RIGHT], RIGHT: xdev[LEFT], OPP: xdev[OPP]}[slot]
            send(k + slot - 1, lambda x_to=x_to: ostage.at[i, lax.rem(x_to, RING)], oall.at[i, slot], to, None)

    def project(l, i, slot, k, reduce):
        for source in (LEFT, RIGHT, OPP):
            arrived(k + source - 1, oall.at[i, source])
        o_all = oall[i].reshape(RING * head_dim, block)
        tile = 1024

        def body(j, carry):
            cols = pl.ds(pl.multiple_of(j * tile, tile), tile)
            w_all = wot[l, :, :, cols].reshape(RING * head_dim, tile)
            reduce.put(slot, cols, dot(o_all, w_all, ((0,), (0,))))
            return carry

        lax.fori_loop(0, width // tile, body, 0)
        reduce.give(slot)

    def mlp_up(l, s, n=1):
        def up(j, carry):
            rows_in = xg_m[s:s + n].reshape(n * block, width)
            h = jax.nn.gelu(dot(rows_in, wu[l, j]), approximate=True).astype(jnp.bfloat16)
            hid[s:s + n, :, pl.ds(pl.multiple_of(j * wu.shape[3], wu.shape[3]), wu.shape[3])] = h.reshape(n, block, wu.shape[3])
            return carry

        lax.fori_loop(0, RING, up, 0)

    def mlp_down(l, s, reduce, n=1):
        tile = 512

        def down(j, carry):
            cols = pl.ds(pl.multiple_of(j * tile, tile), tile)
            w_all = wd[l, :, :, cols].reshape(hid.shape[2], tile)
            term = dot(hid[s:s + n].reshape(n * block, hid.shape[2]), w_all)
            for i in range(n):
                reduce.put(s + i, cols, term[i * block:(i + 1) * block])
            return carry

        lax.fori_loop(0, width // tile, down, 0)
        for i in range(n):
            reduce.give(s + i)

    def scoped(name, fn, *args):
        with jax.named_scope(name):
            return fn(*args)

    for l in range(layers):
        first, last = l == 0, l + 1 == layers
        scoped("drain", drain)
        gather = Gather(xg_a, ydev)
        xg_a[OWN, core] = layer_norm(res[...].astype(jnp.float32), g1_ref[l, :][None, :])
        gather.start()
        heads, receive = attention_front(l, gather)
        near = (OWN, LEFT, RIGHT)
        if first:
            w_q[l].start()
            w_q[l].start_rest()
            scoped("ag_relay", gather.relay)
            scoped("wq_relay", w_q[l].relay)
            scoped("ag_near", gather.near)
            w_u[l].start()
            w_u[l].start_rest()
            scoped("ag_far", gather.far)
            for i in range(2):
                copies[i].wait()
            scoped("wq_near", w_q[l].wait_near)
            for s in (*near, OPP):
                scoped("ag_wait", gather.wait, s)
                scoped("qkv", heads, s, near)
            scoped("wq_far", w_q[l].wait_far)
            for s in (*near, OPP):
                scoped("qkv", heads, s, (OPP,))
            w_o[l].start()
            w_o[l].start_rest()
        else:
            scoped("wq_near", w_q[l].wait_near)
            scoped("wq_far", w_q[l].wait_far)
            scoped("ag_wait", gather.wait, OWN)
            scoped("qkv", heads, OWN, (*near, OPP))
            scoped("ag_relay", gather.relay)
            scoped("ag_near", gather.near)
            w_o[l].start()
            w_o[l].start_rest()
            scoped("ag_wait", gather.wait, LEFT)
            scoped("qkv", heads, LEFT, (*near, OPP))
            scoped("ag_wait", gather.wait, RIGHT)
            scoped("qkv", heads, RIGHT, (*near, OPP))
            scoped("ag_far", gather.far)
            scoped("ag_wait", gather.wait, OPP)
            scoped("qkv", heads, OPP, (*near, OPP))
        scoped("wu_relay", w_u[l].relay)
        w_d[l].start()
        scoped("a2a_wait", receive)
        scoped("drain", drain)
        scoped("keys", prepare_keys)
        k_o = ids.take(3 * RING)
        reduce = Reduce(ydev)
        order = (OPP, LEFT, RIGHT, OWN)

        def finish_segment(i):
            project(l, i, order[i], k_o + 3 * i, reduce)

        def segment(i, carry):
            shift = lax.rem(2 + i + lax.div(i, 2) * (5 - 2 * i), RING)
            scoped("attend", attend, shift, i)
            exchange_o(i, k_o + 3 * i)

            @pl.when(i == 0)
            def _():
                scoped("wo_relay", w_o[l].relay)

            @pl.when(i == 1)
            def _():
                scoped("wo_near", w_o[l].wait_near)
                scoped("wo_far", w_o[l].wait_far)
                scoped("proj", finish_segment, 0)

            @pl.when(i == 2)
            def _():
                scoped("rs_far", reduce.far)
                scoped("proj", finish_segment, 1)

            return carry

        lax.fori_loop(0, RING, segment, 0)
        for i in range(RING):
            for slot, x_to in ((LEFT, xpos + 1), (RIGHT, xpos + 3), (OPP, xpos + 2)):
                pending[k_o + 3 * i + slot - 1] = lambda i=i, x_to=x_to: ostage.at[i, lax.rem(x_to, RING)]
        if not last:
            w_q[l + 1].start()
            w_q[l + 1].start_rest()
        scoped("proj", finish_segment, 2)
        scoped("rs_near", reduce.near, LEFT)
        scoped("proj", finish_segment, 3)
        scoped("rs_near", reduce.near, RIGHT)
        scoped("rs_relay", reduce.relay)
        w_d[l].start_rest()
        scoped("wd_relay", w_d[l].relay)
        if not last:
            scoped("wq_relay", w_q[l + 1].relay)
        scoped("rs_finish", reduce.finish)
        scoped("drain", drain)

        gather = Gather(xg_m, xdev)
        xg_m[OWN, core] = layer_norm(res[...].astype(jnp.float32), g2_ref[l, :][None, :])
        gather.start()
        if not last:
            w_u[l + 1].start()
            w_u[l + 1].start_rest()
        if first:
            for i in range(2, len(copies)):
                copies[i].wait()
        reduce = Reduce(xdev)
        scoped("wu_near", w_u[l].wait_near)
        scoped("wu_far", w_u[l].wait_far)
        scoped("ag_wait", gather.wait, OWN)
        scoped("up", mlp_up, l, OWN)
        scoped("ag_relay", gather.relay)
        scoped("ag_near", gather.near)
        scoped("ag_wait", gather.wait, LEFT)
        scoped("ag_wait", gather.wait, RIGHT)
        scoped("up", mlp_up, l, LEFT, 2)
        scoped("ag_far", gather.far)
        scoped("ag_wait", gather.wait, OPP)
        scoped("up", mlp_up, l, OPP)
        scoped("wd_near", w_d[l].wait_near)
        scoped("wd_far", w_d[l].wait_far)
        scoped("down", mlp_down, l, OPP, reduce)
        scoped("down", mlp_down, l, LEFT, reduce, 2)
        scoped("rs_far", reduce.far)
        scoped("down", mlp_down, l, OWN, reduce)
        scoped("rs_near", reduce.near, LEFT)
        scoped("rs_near", reduce.near, RIGHT)
        scoped("rs_relay", reduce.relay)
        scoped("rs_finish", reduce.finish)
    drain()
    drain(pending_weights)
    out_ref[...] = res[...]


def solution(mesh):
    def layer_stack(x_local, ln1_gain, w_qkv, w_out, ln2_gain, w_up, w_down):
        batch, rows, width = x_local.shape
        layers, _, _, three_e = w_qkv.shape
        head_dim = three_e // 3
        ff = w_up.shape[2]
        block = CORES * rows
        wqt = w_qkv.reshape(layers, width, three_e).transpose(0, 2, 1)
        wo = w_out.reshape(layers, head_dim, width)
        bf16, f32 = jnp.bfloat16, jnp.float32
        vmem = pltpu.VMEM
        n_ids = 200
        hbm = pl.BlockSpec(memory_space=pltpu.HBM)
        in_vmem = pl.BlockSpec(memory_space=pltpu.VMEM)
        scratch = [
            vmem((RING, CORES, rows, width), bf16),
            vmem((RING, CORES, rows, width), bf16),
            vmem((layers, RING, three_e, width), bf16),
            vmem((layers, RING, head_dim, width), bf16),
            vmem((layers, RING, width, ff), bf16),
            vmem((layers, RING, ff, width), bf16),
            vmem((RING, RING - 1, three_e, block), bf16),
            vmem((RING * RING, three_e, block), bf16),
            vmem((RING * RING * block, head_dim), bf16),
            vmem((RING, head_dim, RING * block), bf16),
            vmem((RING, RING, head_dim, block), bf16),
            vmem((RING, RING * block, block), f32),
            vmem((RING, head_dim, block), f32),
            vmem((RING, RING, head_dim, block), bf16),
            vmem((RING, rows, width), f32),
            vmem((RING, rows, width), bf16),
            vmem((RING, rows, width), bf16),
            vmem((2, rows // 2, width), bf16),
            vmem((6, rows // 2, width), bf16),
            vmem((2, 2, rows // 2, width), bf16),
            vmem((RING, block, RING * ff), bf16),
            vmem((rows, width), bf16),
            pltpu.SemaphoreType.DMA((n_ids,)),
            pltpu.SemaphoreType.DMA((n_ids,)),
            pltpu.SemaphoreType.DMA((4 * layers,)),
        ]

        def kernel(*refs):
            ids = Ids()
            stack_kernel(layers, *refs, ids)
            assert ids.count <= n_ids, ids.count

        out = pl.pallas_call(
            kernel,
            out_shape=jax.ShapeDtypeStruct((rows, width), bf16),
            in_specs=[in_vmem, in_vmem, in_vmem, hbm, hbm, hbm, hbm],
            out_specs=in_vmem,
            scratch_shapes=scratch,
            compiler_params=pltpu.CompilerParams(collective_id=0, has_side_effects=True, vmem_limit_bytes=VMEM_LIMIT),
        )(x_local.reshape(rows, width), ln1_gain, ln2_gain, wqt, wo, w_up, w_down)
        return out.reshape(batch, rows, width)

    return jax.shard_map(layer_stack, mesh=mesh, in_specs=(P('dp', 'tp', None), P(), P(None, None, 'tp', None), P(None, 'tp', None, None), P(), P(None, None, 'tp'), P(None, 'tp', None)), out_specs=P('dp', 'tp', None), check_vma=False)
```

time: 339 us -> 270 us (0.80); the launches traced: 334 us -> 270 us
  Pallas kernels: 332 us -> 268 us
    pallas_call x1, Pallas kernels: 332 us -> 268 us  [layer_stack(): pl.pallas_call(kernel, out_shape=jax.ShapeDtypeStruct((rows, width), bf16...]
where the time goes in v2:
time: 270 us
  Pallas kernels  268 us (99%)
    pallas_call x1, Pallas kernels, layer_stack(): pl.pallas_call(kernel, out_shape=jax.ShapeDtypeStruct((rows, width), bf16...  268 us

profile of v2, /device:TPU:97, one launch (start us, length us, event | category | flops | bytes accessed | tf_op | source)
XLA Modules:
  0.0 270.2 jit_solution(14613379269019849765)
XLA Ops:
  0.0 268.3 %shard_map.73 = bf16[128,2048]{1,0:T(8,128)(2,1)} custom-call(bf16[128,2048]{1,0:T(8,128)(2,1)} %bitcast.8, f32[2,2048]{1,0:T(2,128)} %refs_1_.1, f32[2,2048]{1,0:T(2,128)} %refs_2_.1, bf16[2,192,2048]{2,1,0:T(8,128)(2,1)} %bitcast.7, bf16[2,64,2048]{2,1,0:T(8,128)(2,1)} %bitcast.9, bf16[2,2048,256]{2,1,0:T(8,128)(2,1)} %refs_5_.1, bf16[2,256,2048]{2,1,0:T(8,128)(2,1)} %refs_6_.1), custom_call_target="tpu_custom_call" | custom-call | tf_op jit(solution)/shard_map/pallas_call | solution.py:532
  268.3 1.9 copy.9

commit v3 on v2

--- a/solution.py
+++ b/solution.py
@@ -58,7 +58,7 @@
     xdev = {LEFT: dev(ypos, xpos + 3, core), RIGHT: dev(ypos, xpos + 1, core), OPP: dev(ypos, xpos + 2, core)}
     ydev = {LEFT: dev(ypos + 3, xpos, core), RIGHT: dev(ypos + 1, xpos, core)}
 
-    pending, pending_weights = {}, {}
+    pending, pending_weights, pending_early = {}, {}, {}
 
     def send(k, src, dst, device, queue=pending):
         copy = pltpu.make_async_remote_copy(src_ref=src(), dst_ref=dst, send_sem=send_sem.at[k], recv_sem=recv_sem.at[k],
@@ -79,7 +79,7 @@
 
     class Gather:
         def __init__(self, buf, ring):
-            self.buf, self.ring, self.k = buf, ring, ids.take(12)
+            self.buf, self.ring, self.k = buf, ring, ids.take(10)
             self.a, self.b = pl.ds(0, half), pl.ds(half, half)
 
         def start(self):
@@ -112,9 +112,8 @@
             arrived(self.k + {OWN: 2, LEFT: 7, RIGHT: 8, OPP: 9}[slot], self.buf.at[slot, other])
 
     class Weights:
-        def __init__(self, src, buf, ring):
-            self.src, self.buf, self.ring = src, buf, ring
-            self.k = ids.take(6)
+        def __init__(self, src, buf, ring, k, queue):
+            self.src, self.buf, self.ring, self.k, self.queue = src, buf, ring, k, queue
             n = buf.shape[1] // 2
             self.a, self.b = pl.ds(0, n), pl.ds(n, n)
 
@@ -125,19 +124,19 @@
 
         def start(self):
             right, left = self.ring[RIGHT], self.ring[LEFT]
-            send(self.k, lambda: self.src.at[self.a], self.buf.at[LEFT, self.a], right, pending_weights)
-            send(self.k + 1, lambda: self.src.at[self.b], self.buf.at[RIGHT, self.b], left, pending_weights)
+            send(self.k, lambda: self.src.at[self.a], self.buf.at[LEFT, self.a], right, self.queue)
+            send(self.k + 1, lambda: self.src.at[self.b], self.buf.at[RIGHT, self.b], left, self.queue)
 
         def start_rest(self):
             right, left = self.ring[RIGHT], self.ring[LEFT]
-            send(self.k + 2, lambda: self.src.at[self.b], self.buf.at[LEFT, self.b], right, pending_weights)
-            send(self.k + 3, lambda: self.src.at[self.a], self.buf.at[RIGHT, self.a], left, pending_weights)
+            send(self.k + 2, lambda: self.src.at[self.b], self.buf.at[LEFT, self.b], right, self.queue)
+            send(self.k + 3, lambda: self.src.at[self.a], self.buf.at[RIGHT, self.a], left, self.queue)
 
         def relay(self):
             arrived(self.k, self.buf.at[LEFT, self.a])
-            send(self.k + 4, lambda: self.buf.at[LEFT, self.a], self.buf.at[OPP, self.a], self.ring[RIGHT], pending_weights)
+            send(self.k + 4, lambda: self.buf.at[LEFT, self.a], self.buf.at[OPP, self.a], self.ring[RIGHT], self.queue)
             arrived(self.k + 1, self.buf.at[RIGHT, self.b])
-            send(self.k + 5, lambda: self.buf.at[RIGHT, self.b], self.buf.at[OPP, self.b], self.ring[LEFT], pending_weights)
+            send(self.k + 5, lambda: self.buf.at[RIGHT, self.b], self.buf.at[OPP, self.b], self.ring[LEFT], self.queue)
 
         def wait_near(self):
             arrived(self.k + 2, self.buf.at[LEFT, self.b])
@@ -200,10 +199,11 @@
                 total = self.term(OWN, part) + direct[0, i].astype(jnp.float32) + direct[1, i].astype(jnp.float32)
                 res[part, :] = (res[part, :].astype(jnp.float32) + total).astype(jnp.bfloat16)
 
-    w_q = [Weights(wqt_ref.at[l], wq.at[l], xdev) for l in range(layers)]
-    w_o = [Weights(wo_ref.at[l], wot.at[l], xdev) for l in range(layers)]
-    w_u = [Weights(wu_ref.at[l], wu.at[l], ydev) for l in range(layers)]
-    w_d = [Weights(wd_ref.at[l], wd.at[l], ydev) for l in range(layers)]
+    k_q, k_w = ids.take(6), ids.take(6)
+    w_q = [Weights(wqt_ref.at[l], wq.at[l], xdev, k_q, pending_early) for l in range(layers)]
+    w_o = [Weights(wo_ref.at[l], wot.at[l], xdev, k_w, pending_early) for l in range(layers)]
+    w_u = [Weights(wu_ref.at[l], wu.at[l], ydev, ids.take(6), pending_weights) for l in range(layers)]
+    w_d = [Weights(wd_ref.at[l], wd.at[l], ydev, ids.take(6), pending_weights) for l in range(layers)]
     everything = [w for l in range(layers) for w in (w_q[l], w_o[l], w_u[l], w_d[l])]
     copies = [w.local(i) for i, w in enumerate(everything)]
 
@@ -220,8 +220,6 @@
 
     def attention_front(l, gather):
         k = ids.take(3 * RING)
-        order = (OWN, LEFT, RIGHT, OPP)
-
         def heads(s, slots):
             rows_in = xg_a[s].reshape(CORES * rows, width)
             n = len(slots)
@@ -236,24 +234,25 @@
                     stage[s, slot - 1] = part[i]
                     send(k + 3 * s + slot - 1, lambda slot=slot: stage.at[s, slot - 1], qkv.at[g], xdev[slot])
 
-        def receive():
-            for s in order:
-                shift = {OWN: 0, LEFT: 3, RIGHT: 1, OPP: 2}[s]
-                for slot in (LEFT, RIGHT, OPP):
-                    x_from = {LEFT: xpos + 1, RIGHT: xpos + 3, OPP: xpos + 2}[slot]
-                    g = lax.rem(ypos + shift, RING) * RING + lax.rem(x_from, RING)
-                    arrived(k + 3 * s + slot - 1, qkv.at[g])
+        def receive(s):
+            shift = {OWN: 0, LEFT: 3, RIGHT: 1, OPP: 2}[s]
+            y = lax.rem(ypos + shift, RING)
+            for slot in (LEFT, RIGHT, OPP):
+                x_from = {LEFT: xpos + 1, RIGHT: xpos + 3, OPP: xpos + 2}[slot]
+                arrived(k + 3 * s + slot - 1, qkv.at[y * RING + lax.rem(x_from, RING)])
+            return y
 
         return heads, receive
 
-    def prepare_keys():
-        def body(g, carry):
+    def prepare_keys(y):
+        def body(x, carry):
+            g = y * RING + x
             keys[pl.ds(pl.multiple_of(g * block, block), block), :] = (
                 qkv[g, head_dim:2 * head_dim, :].astype(jnp.float32).T.astype(jnp.bfloat16))
-            vals[g // RING, :, pl.ds(pl.multiple_of(lax.rem(g, RING) * block, block), block)] = qkv[g, 2 * head_dim:, :]
+            vals[y, :, pl.ds(pl.multiple_of(x * block, block), block)] = qkv[g, 2 * head_dim:, :]
             return carry
 
-        lax.fori_loop(0, RING * RING, body, 0)
+        lax.fori_loop(0, RING, body, 0)
 
     def attend(shift, i):
         y = lax.rem(ypos + shift, RING)
@@ -348,9 +347,11 @@
         with jax.named_scope(name):
             return fn(*args)
 
+    first_id = ids.count
     for l in range(layers):
+        ids.count = first_id
         first, last = l == 0, l + 1 == layers
-        scoped("drain", drain)
+        drain()
         gather = Gather(xg_a, ydev)
         xg_a[OWN, core] = layer_norm(res[...].astype(jnp.float32), g1_ref[l, :][None, :])
         gather.start()
@@ -377,14 +378,15 @@
             w_o[l].start()
             w_o[l].start_rest()
         else:
+            w_o[l].start()
+            w_o[l].start_rest()
             scoped("wq_near", w_q[l].wait_near)
             scoped("wq_far", w_q[l].wait_far)
             scoped("ag_wait", gather.wait, OWN)
             scoped("qkv", heads, OWN, (*near, OPP))
             scoped("ag_relay", gather.relay)
+            scoped("wo_relay", w_o[l].relay)
             scoped("ag_near", gather.near)
-            w_o[l].start()
-            w_o[l].start_rest()
             scoped("ag_wait", gather.wait, LEFT)
             scoped("qkv", heads, LEFT, (*near, OPP))
             scoped("ag_wait", gather.wait, RIGHT)
@@ -392,11 +394,17 @@
             scoped("ag_far", gather.far)
             scoped("ag_wait", gather.wait, OPP)
             scoped("qkv", heads, OPP, (*near, OPP))
-        scoped("wu_relay", w_u[l].relay)
+        if first:
+            scoped("wu_relay", w_u[l].relay)
         w_d[l].start()
-        scoped("a2a_wait", receive)
+        if not first:
+            w_d[l].start_rest()
+        for s in (*near, OPP):
+            y = scoped("a2a_wait", receive, s)
+            scoped("keys", prepare_keys, y)
+        if first:
+            scoped("wo_relay", w_o[l].relay)
         scoped("drain", drain)
-        scoped("keys", prepare_keys)
         k_o = ids.take(3 * RING)
         reduce = Reduce(ydev)
         order = (OPP, LEFT, RIGHT, OWN)
@@ -408,10 +416,6 @@
             shift = lax.rem(2 + i + lax.div(i, 2) * (5 - 2 * i), RING)
             scoped("attend", attend, shift, i)
             exchange_o(i, k_o + 3 * i)
-
-            @pl.when(i == 0)
-            def _():
-                scoped("wo_relay", w_o[l].relay)
 
             @pl.when(i == 1)
             def _():
@@ -431,17 +435,17 @@
             for slot, x_to in ((LEFT, xpos + 1), (RIGHT, xpos + 3), (OPP, xpos + 2)):
                 pending[k_o + 3 * i + slot - 1] = lambda i=i, x_to=x_to: ostage.at[i, lax.rem(x_to, RING)]
         if not last:
+            drain(pending_early)
             w_q[l + 1].start()
             w_q[l + 1].start_rest()
         scoped("proj", finish_segment, 2)
         scoped("rs_near", reduce.near, LEFT)
+        scoped("rs_near", reduce.near, RIGHT)
         scoped("proj", finish_segment, 3)
-        scoped("rs_near", reduce.near, RIGHT)
         scoped("rs_relay", reduce.relay)
-        w_d[l].start_rest()
+        if first:
+            w_d[l].start_rest()
         scoped("wd_relay", w_d[l].relay)
-        if not last:
-            scoped("wq_relay", w_q[l + 1].relay)
         scoped("rs_finish", reduce.finish)
         scoped("drain", drain)
 
@@ -461,23 +465,40 @@
         scoped("up", mlp_up, l, OWN)
         scoped("ag_relay", gather.relay)
         scoped("ag_near", gather.near)
+        if not first:
+            scoped("wd_near", w_d[l].wait_near)
+            scoped("wd_far", w_d[l].wait_far)
+            scoped("down", mlp_down, l, OWN, reduce)
         scoped("ag_wait", gather.wait, LEFT)
         scoped("ag_wait", gather.wait, RIGHT)
         scoped("up", mlp_up, l, LEFT, 2)
         scoped("ag_far", gather.far)
+        if not first:
+            scoped("down", mlp_down, l, LEFT, reduce, 2)
         scoped("ag_wait", gather.wait, OPP)
+        if not last:
+            scoped("wq_relay", w_q[l + 1].relay)
         scoped("up", mlp_up, l, OPP)
-        scoped("wd_near", w_d[l].wait_near)
-        scoped("wd_far", w_d[l].wait_far)
-        scoped("down", mlp_down, l, OPP, reduce)
-        scoped("down", mlp_down, l, LEFT, reduce, 2)
-        scoped("rs_far", reduce.far)
-        scoped("down", mlp_down, l, OWN, reduce)
-        scoped("rs_near", reduce.near, LEFT)
-        scoped("rs_near", reduce.near, RIGHT)
+        if first:
+            scoped("wd_near", w_d[l].wait_near)
+            scoped("wd_far", w_d[l].wait_far)
+            scoped("down", mlp_down, l, OPP, reduce)
+            scoped("down", mlp_down, l, LEFT, reduce, 2)
+            scoped("rs_far", reduce.far)
+            scoped("rs_near", reduce.near, LEFT)
+            scoped("rs_near", reduce.near, RIGHT)
+            scoped("down", mlp_down, l, OWN, reduce)
+        else:
+            scoped("rs_near", reduce.near, LEFT)
+            scoped("rs_near", reduce.near, RIGHT)
+            scoped("down", mlp_down, l, OPP, reduce)
+            scoped("rs_far", reduce.far)
         scoped("rs_relay", reduce.relay)
+        if not last:
+            scoped("wu_relay", w_u[l + 1].relay)
         scoped("rs_finish", reduce.finish)
     drain()
+    drain(pending_early)
     drain(pending_weights)
     out_ref[...] = res[...]
 
@@ -493,7 +514,7 @@
         wo = w_out.reshape(layers, head_dim, width)
         bf16, f32 = jnp.bfloat16, jnp.float32
         vmem = pltpu.VMEM
-        n_ids = 200
+        n_ids = 12 + 12 * layers + 64
         hbm = pl.BlockSpec(memory_space=pltpu.HBM)
         in_vmem = pl.BlockSpec(memory_space=pltpu.VMEM)
         scratch = [

time: 270 us -> 260 us (0.963)
  Pallas kernels: 268 us -> 257 us
    pallas_call x1, Pallas kernels: 268 us -> 257 us  [layer_stack(): pl.pallas_call(kernel, out_shape=jax.ShapeDtypeStruct((rows, width), bf16...]
where the time goes in v3:
time: 260 us; the launch traced here: 259 us
  Pallas kernels  257 us (99%)
    pallas_call x1, Pallas kernels, layer_stack(): pl.pallas_call(kernel, out_shape=jax.ShapeDtypeStruct((rows, width), bf16...  257 us

profile of v3, /device:TPU:97, one launch (start us, length us, event | category | flops | bytes accessed | tf_op | source)
XLA Modules:
  0.0 259.4 jit_solution(4345172057101002404)
XLA Ops:
  0.0 257.5 %shard_map.73 = bf16[128,2048]{1,0:T(8,128)(2,1)} custom-call(bf16[128,2048]{1,0:T(8,128)(2,1)} %bitcast.8, f32[2,2048]{1,0:T(2,128)} %refs_1_.1, f32[2,2048]{1,0:T(2,128)} %refs_2_.1, bf16[2,192,2048]{2,1,0:T(8,128)(2,1)} %bitcast.7, bf16[2,64,2048]{2,1,0:T(8,128)(2,1)} %bitcast.9, bf16[2,2048,256]{2,1,0:T(8,128)(2,1)} %refs_5_.1, bf16[2,256,2048]{2,1,0:T(8,128)(2,1)} %refs_6_.1), custom_call_target="tpu_custom_call" | custom-call | tf_op jit(solution)/shard_map/pallas_call | solution.py:553
  257.5 1.9 copy.9

commit v4 on v3

--- a/solution.py
+++ b/solution.py
@@ -79,7 +79,7 @@
 
     class Gather:
         def __init__(self, buf, ring):
-            self.buf, self.ring, self.k = buf, ring, ids.take(10)
+            self.buf, self.ring, self.k = buf, ring, ids.take(12)
             self.a, self.b = pl.ds(0, half), pl.ds(half, half)
 
         def start(self):
@@ -94,14 +94,16 @@
         def relay(self):
             arrived(self.k, self.buf.at[LEFT, core, self.a])
             send(self.k + 5, lambda: self.buf.at[LEFT, core, self.a], self.buf.at[OPP, core, self.a], self.ring[RIGHT])
+            send(self.k + 7, lambda: self.buf.at[LEFT, core, self.a], self.buf.at[LEFT, core, self.a], partner)
             arrived(self.k + 1, self.buf.at[RIGHT, core, self.b])
             send(self.k + 6, lambda: self.buf.at[RIGHT, core, self.b], self.buf.at[OPP, core, self.b], self.ring[LEFT])
+            send(self.k + 8, lambda: self.buf.at[RIGHT, core, self.b], self.buf.at[RIGHT, core, self.b], partner)
 
         def near(self):
             arrived(self.k + 3, self.buf.at[LEFT, core, self.b])
-            send(self.k + 7, lambda: self.buf.at[LEFT, core], self.buf.at[LEFT, core], partner)
+            send(self.k + 10, lambda: self.buf.at[LEFT, core, self.b], self.buf.at[LEFT, core, self.b], partner)
             arrived(self.k + 4, self.buf.at[RIGHT, core, self.a])
-            send(self.k + 8, lambda: self.buf.at[RIGHT, core], self.buf.at[RIGHT, core], partner)
+            send(self.k + 11, lambda: self.buf.at[RIGHT, core, self.a], self.buf.at[RIGHT, core, self.a], partner)
 
         def far(self):
             arrived(self.k + 5, self.buf.at[OPP, core, self.a])
@@ -109,7 +111,12 @@
             send(self.k + 9, lambda: self.buf.at[OPP, core], self.buf.at[OPP, core], partner)
 
         def wait(self, slot):
-            arrived(self.k + {OWN: 2, LEFT: 7, RIGHT: 8, OPP: 9}[slot], self.buf.at[slot, other])
+            if slot in (OWN, OPP):
+                arrived(self.k + {OWN: 2, OPP: 9}[slot], self.buf.at[slot, other])
+            else:
+                first, second = {LEFT: (self.a, self.b), RIGHT: (self.b, self.a)}[slot]
+                arrived(self.k + {LEFT: 7, RIGHT: 8}[slot], self.buf.at[slot, other, first])
+                arrived(self.k + {LEFT: 10, RIGHT: 11}[slot], self.buf.at[slot, other, second])
 
     class Weights:
         def __init__(self, src, buf, ring, k, queue):
@@ -326,7 +333,7 @@
             hid[s:s + n, :, pl.ds(pl.multiple_of(j * wu.shape[3], wu.shape[3]), wu.shape[3])] = h.reshape(n, block, wu.shape[3])
             return carry
 
-        lax.fori_loop(0, RING, up, 0)
+        lax.fori_loop(0, RING, up, 0, unroll=2)
 
     def mlp_down(l, s, reduce, n=1):
         tile = 512
@@ -339,7 +346,7 @@
                 reduce.put(s + i, cols, term[i * block:(i + 1) * block])
             return carry
 
-        lax.fori_loop(0, width // tile, down, 0)
+        lax.fori_loop(0, width // tile, down, 0, unroll=2)
         for i in range(n):
             reduce.give(s + i)
 
@@ -392,18 +399,15 @@
             scoped("ag_wait", gather.wait, RIGHT)
             scoped("qkv", heads, RIGHT, (*near, OPP))
             scoped("ag_far", gather.far)
+            scoped("wu_relay", w_u[l].relay)
             scoped("ag_wait", gather.wait, OPP)
             scoped("qkv", heads, OPP, (*near, OPP))
         if first:
             scoped("wu_relay", w_u[l].relay)
         w_d[l].start()
-        if not first:
-            w_d[l].start_rest()
         for s in (*near, OPP):
             y = scoped("a2a_wait", receive, s)
             scoped("keys", prepare_keys, y)
-        if first:
-            scoped("wo_relay", w_o[l].relay)
         scoped("drain", drain)
         k_o = ids.take(3 * RING)
         reduce = Reduce(ydev)
@@ -417,16 +421,17 @@
             scoped("attend", attend, shift, i)
             exchange_o(i, k_o + 3 * i)
 
-            @pl.when(i == 1)
+            if first:
+                @pl.when(i == 0)
+                def _():
+                    scoped("wo_relay", w_o[l].relay)
+
+            @pl.when(i == 2)
             def _():
                 scoped("wo_near", w_o[l].wait_near)
                 scoped("wo_far", w_o[l].wait_far)
                 scoped("proj", finish_segment, 0)
-
-            @pl.when(i == 2)
-            def _():
                 scoped("rs_far", reduce.far)
-                scoped("proj", finish_segment, 1)
 
             return carry
 
@@ -438,13 +443,13 @@
             drain(pending_early)
             w_q[l + 1].start()
             w_q[l + 1].start_rest()
+        scoped("proj", finish_segment, 1)
         scoped("proj", finish_segment, 2)
         scoped("rs_near", reduce.near, LEFT)
         scoped("rs_near", reduce.near, RIGHT)
         scoped("proj", finish_segment, 3)
         scoped("rs_relay", reduce.relay)
-        if first:
-            w_d[l].start_rest()
+        w_d[l].start_rest()
         scoped("wd_relay", w_d[l].relay)
         scoped("rs_finish", reduce.finish)
         scoped("drain", drain)
@@ -465,15 +470,13 @@
         scoped("up", mlp_up, l, OWN)
         scoped("ag_relay", gather.relay)
         scoped("ag_near", gather.near)
-        if not first:
-            scoped("wd_near", w_d[l].wait_near)
-            scoped("wd_far", w_d[l].wait_far)
-            scoped("down", mlp_down, l, OWN, reduce)
         scoped("ag_wait", gather.wait, LEFT)
         scoped("ag_wait", gather.wait, RIGHT)
         scoped("up", mlp_up, l, LEFT, 2)
         scoped("ag_far", gather.far)
         if not first:
+            scoped("wd_near", w_d[l].wait_near)
+            scoped("wd_far", w_d[l].wait_far)
             scoped("down", mlp_down, l, LEFT, reduce, 2)
         scoped("ag_wait", gather.wait, OPP)
         if not last:
@@ -493,9 +496,8 @@
             scoped("rs_near", reduce.near, RIGHT)
             scoped("down", mlp_down, l, OPP, reduce)
             scoped("rs_far", reduce.far)
+            scoped("down", mlp_down, l, OWN, reduce)
         scoped("rs_relay", reduce.relay)
-        if not last:
-            scoped("wu_relay", w_u[l + 1].relay)
         scoped("rs_finish", reduce.finish)
     drain()
     drain(pending_early)
@@ -514,7 +516,7 @@
         wo = w_out.reshape(layers, head_dim, width)
         bf16, f32 = jnp.bfloat16, jnp.float32
         vmem = pltpu.VMEM
-        n_ids = 12 + 12 * layers + 64
+        n_ids = 12 + 12 * layers + 68
         hbm = pl.BlockSpec(memory_space=pltpu.HBM)
         in_vmem = pl.BlockSpec(memory_space=pltpu.VMEM)
         scratch = [

time: 260 us -> 256 us (0.985)
  Pallas kernels: 257 us -> 254 us
    pallas_call x1, Pallas kernels: 257 us -> 254 us  [layer_stack(): pl.pallas_call(kernel, out_shape=jax.ShapeDtypeStruct((rows, width), bf16...]
where the time goes in v4:
time: 256 us
  Pallas kernels  254 us (99%)
    pallas_call x1, Pallas kernels, layer_stack(): pl.pallas_call(kernel, out_shape=jax.ShapeDtypeStruct((rows, width), bf16...  254 us

profile of v4, /device:TPU:97, one launch (start us, length us, event | category | flops | bytes accessed | tf_op | source)
XLA Modules:
  0.0 255.8 jit_solution(12138976240947895411)
XLA Ops:
  0.0 253.9 %shard_map.73 = bf16[128,2048]{1,0:T(8,128)(2,1)} custom-call(bf16[128,2048]{1,0:T(8,128)(2,1)} %bitcast.8, f32[2,2048]{1,0:T(2,128)} %refs_1_.1, f32[2,2048]{1,0:T(2,128)} %refs_2_.1, bf16[2,192,2048]{2,1,0:T(8,128)(2,1)} %bitcast.7, bf16[2,64,2048]{2,1,0:T(8,128)(2,1)} %bitcast.9, bf16[2,2048,256]{2,1,0:T(8,128)(2,1)} %refs_5_.1, bf16[2,256,2048]{2,1,0:T(8,128)(2,1)} %refs_6_.1), custom_call_target="tpu_custom_call" | custom-call | tf_op jit(solution)/shard_map/pallas_call | solution.py:555
  253.9 1.9 copy.9

commit v5 on v4

--- a/solution.py
+++ b/solution.py
@@ -219,6 +219,7 @@
     for peer in peers:
         pl.semaphore_signal(barrier, inc=1, device_id={"dp": part, "tp": peer}, device_id_type=MESH)
     res[...] = x_ref[...]
+    xg_a[OWN, core] = layer_norm(res[...].astype(jnp.float32), g1_ref[0, :][None, :])
     pl.semaphore_wait(barrier, len(peers))
 
     head_dim = keys.shape[1]
@@ -360,7 +361,8 @@
         first, last = l == 0, l + 1 == layers
         drain()
         gather = Gather(xg_a, ydev)
-        xg_a[OWN, core] = layer_norm(res[...].astype(jnp.float32), g1_ref[l, :][None, :])
+        if not first:
+            xg_a[OWN, core] = layer_norm(res[...].astype(jnp.float32), g1_ref[l, :][None, :])
         gather.start()
         heads, receive = attention_front(l, gather)
         near = (OWN, LEFT, RIGHT)
@@ -387,13 +389,13 @@
         else:
             w_o[l].start()
             w_o[l].start_rest()
+            scoped("ag_relay", gather.relay)
             scoped("wq_near", w_q[l].wait_near)
             scoped("wq_far", w_q[l].wait_far)
             scoped("ag_wait", gather.wait, OWN)
             scoped("qkv", heads, OWN, (*near, OPP))
-            scoped("ag_relay", gather.relay)
+            scoped("ag_near", gather.near)
             scoped("wo_relay", w_o[l].relay)
-            scoped("ag_near", gather.near)
             scoped("ag_wait", gather.wait, LEFT)
             scoped("qkv", heads, LEFT, (*near, OPP))
             scoped("ag_wait", gather.wait, RIGHT)
@@ -479,8 +481,6 @@
             scoped("wd_far", w_d[l].wait_far)
             scoped("down", mlp_down, l, LEFT, reduce, 2)
         scoped("ag_wait", gather.wait, OPP)
-        if not last:
-            scoped("wq_relay", w_q[l + 1].relay)
         scoped("up", mlp_up, l, OPP)
         if first:
             scoped("wd_near", w_d[l].wait_near)
@@ -498,6 +498,8 @@
             scoped("rs_far", reduce.far)
             scoped("down", mlp_down, l, OWN, reduce)
         scoped("rs_relay", reduce.relay)
+        if not last:
+            scoped("wq_relay", w_q[l + 1].relay)
         scoped("rs_finish", reduce.finish)
     drain()
     drain(pending_early)

time: 256 us -> 254 us (level)
  no operation moved by 1% of the time
where the time goes in v5:
time: 254 us
  Pallas kernels  252 us (99%)
    pallas_call x1, Pallas kernels, layer_stack(): pl.pallas_call(kernel, out_shape=jax.ShapeDtypeStruct((rows, width), bf16...  252 us

profile of v5, /device:TPU:97, one launch (start us, length us, event | category | flops | bytes accessed | tf_op | source)
XLA Modules:
  0.0 254.3 jit_solution(17716925109702950654)
XLA Ops:
  0.0 252.4 %shard_map.73 = bf16[128,2048]{1,0:T(8,128)(2,1)} custom-call(bf16[128,2048]{1,0:T(8,128)(2,1)} %bitcast.8, f32[2,2048]{1,0:T(2,128)} %refs_1_.1, f32[2,2048]{1,0:T(2,128)} %refs_2_.1, bf16[2,192,2048]{2,1,0:T(8,128)(2,1)} %bitcast.7, bf16[2,64,2048]{2,1,0:T(8,128)(2,1)} %bitcast.9, bf16[2,2048,256]{2,1,0:T(8,128)(2,1)} %refs_5_.1, bf16[2,256,2048]{2,1,0:T(8,128)(2,1)} %refs_6_.1), custom_call_target="tpu_custom_call" | custom-call | tf_op jit(solution)/shard_map/pallas_call | solution.py:557
  252.4 1.9 copy.9
